TPU v7x, 32 devices: a 4x4x1 block of a 4x4x8 slice. The times are simulated.
32 devices in a mesh: dp: 1 (over z), ep: 4 (over y), tp: 8 (over x, core).
Axes of the slice: x: 4, y: 4, z: 1, core: 2. Of those that a mesh axis runs over, the one named last changes fastest.
The devices are a block of a 4x4x8 slice.
Arguments:
- x_in: bfloat16 [4096, 2048], P(('dp', 'ep'))
- expert_ids: int32 [4096, 2], P(('dp', 'ep'))
- gate_vals: float32 [4096, 2], P(('dp', 'ep'))
- w_gate: bfloat16 [8, 2048, 7168], P('ep', None, 'tp')
- w_up: bfloat16 [8, 2048, 7168], P('ep', None, 'tp')
- w_down: bfloat16 [8, 7168, 2048], P('ep', 'tp')
Outputs:
- output: bfloat16 [4096, 2048], P(('dp', 'ep'))
All inputs are finite; a program needn't handle non-finite values.
Results may differ from a plain program's by a relative error of at most 0.00932271.
Values are sent between devices in bfloat16 or wider.
A program may use at most 768 MiB of HBM per device.

v0:
```python
import jax
import jax.numpy as jnp
from jax import lax
from jax.sharding import PartitionSpec as P

CAP_NUM = 5
CAP_DEN = 4


def local_routing(expert_ids, n_experts, capacity):
    tokens, n_top = expert_ids.shape
    flat_ids = expert_ids.reshape(tokens * n_top)
    onehot = (flat_ids[:, None] == jnp.arange(n_experts, dtype=jnp.int32)[None, :]).astype(jnp.int32)
    slots = jnp.sum((jnp.cumsum(onehot, axis=0) - onehot) * onehot, axis=1)
    flat_slot = jnp.where(slots < capacity, flat_ids * capacity + slots, n_experts * capacity)
    token_num = jnp.broadcast_to(jnp.arange(tokens, dtype=jnp.int32)[:, None], (tokens, n_top)).reshape(tokens * n_top)
    slot_owner = jnp.full((n_experts * capacity + 1,), tokens, jnp.int32).at[flat_slot].set(token_num)
    return slot_owner[: n_experts * capacity].reshape(n_experts, capacity), flat_slot.reshape(tokens, n_top)


def solution(mesh):
    n_ep = mesh.shape['ep']
    n_tp = mesh.shape['tp']
    row_spec = P(('dp', 'ep'), None)

    def device_body(x_loc, ids_loc, gates_loc, wg_loc, wu_loc, wd_loc):
        tokens, d_model = x_loc.shape
        n_top = ids_loc.shape[1]
        local_experts = wg_loc.shape[0]
        n_experts = local_experts * n_ep
        capacity = CAP_NUM * n_top * tokens // (CAP_DEN * n_experts)
        slot_share = capacity // n_tp
        slot_owner, flat_slot = local_routing(ids_loc, n_experts, capacity)
        my_owner = lax.dynamic_slice_in_dim(slot_owner, lax.axis_index('tp') * slot_share, slot_share, axis=1)
        outgoing = jnp.take(x_loc, my_owner, axis=0, mode='fill', fill_value=0)
        outgoing = outgoing.reshape(n_ep, local_experts, slot_share, d_model)
        arrived = lax.all_to_all(outgoing, 'ep', 0, 2, tiled=True).reshape(local_experts, n_ep * slot_share, d_model)
        gathered = lax.all_gather(arrived, 'tp', axis=1, tiled=True)
        h_gate = jnp.einsum('erd,edf->erf', gathered, wg_loc, preferred_element_type=jnp.float32)
        h_up = jnp.einsum('erd,edf->erf', gathered, wu_loc, preferred_element_type=jnp.float32)
        hidden = (jax.nn.silu(h_gate) * h_up).astype(jnp.bfloat16)
        part_out = jnp.einsum('erf,efd->erd', hidden, wd_loc, preferred_element_type=jnp.float32).astype(jnp.bfloat16)
        part_out = part_out.reshape(local_experts, n_tp, n_ep * slot_share, d_model)
        pieces = lax.all_to_all(part_out, 'tp', 1, 1, tiled=True)
        y_mine = jnp.sum(pieces, axis=1, dtype=jnp.float32).astype(jnp.bfloat16)
        returned = lax.all_to_all(y_mine.reshape(local_experts, n_ep, slot_share, d_model), 'ep', 1, 0, tiled=True)
        returned = returned.reshape(n_experts, slot_share, d_model)
        y_all = lax.all_gather(returned, 'tp', axis=1, tiled=True).reshape(n_experts * capacity, d_model)
        picked = jnp.take(y_all, flat_slot, axis=0, mode='fill', fill_value=0)
        return jnp.sum(picked * gates_loc[:, :, None], axis=1).astype(jnp.bfloat16)

    return jax.shard_map(device_body, mesh=mesh,
                         in_specs=(row_spec, row_spec, row_spec, P('ep', None, 'tp'), P('ep', None, 'tp'), P('ep', 'tp', None)),
                         out_specs=row_spec, check_vma=False)
```

profile of v0, /device:TPU:97, one launch (start us, length us, event | category | flops | bytes accessed | tf_op | source)
XLA Modules:
  0.0 451.3 jit_solution(16641842561955958666)
XLA Ops:
  6.5 0.0 all-gather.3.cloned.1.call-start
  6.6 0.9 copy.23
  7.5 0.3 eq.29
  7.7 0.3 eq.25
  8.1 2.3 reduce-window.6
  10.4 0.3 slice_reduce_fusion
  10.6 0.2 reduce-window.9
  10.8 0.1 add_bitcast_fusion
  10.9 0.3 mul.37
  11.3 0.3 reshape.120
  11.6 8.1 %scatter_custom_fusion = s32[2561]{0:T(1024)S(1)} fusion(s32[2048]{0:T(1024)S(1)} %bitcast.59, s32[2048]{0:T(1024)S(1)} %reshape.120, s32[]{:T(128)} %constant.30.clone.1), kind=kCustom, calls=%fused_computation.23 | custom fusion | bytes 10248 | tf_op jit(solution)/shard_map/scatter | solution.py:17
  19.7 0.1 reshape.94
  19.8 0.1 compare_and_fusion.1
  19.8 0.1 reshape.102
  19.9 7.1 %gather_fusion = bf16[320,2048]{1,0:T(8,128)(2,1)S(1)} fusion(bf16[1024,2048]{1,0:T(8,128)(2,1)} %param.6, s32[1024]{0:T(1024)S(1)} %pad_clamp_fusion), kind=kCustom, calls=%fused_computation | custom fusion | bytes 2622720 | tf_op jit(solution)/shard_map/jit(_take)/gather | solution.py:35
  27.0 0.2 broadcast_select_fusion.1
  27.2 23.3 %all_to_all.35 = bf16[4,2,40,2048]{3,2,1,0:T(8,128)(2,1)S(1)} all-to-all(bf16[4,2,40,2048]{3,2,1,0:T(8,128)(2,1)S(1)} %broadcast_select_fusion.1), channel_id=1, replica_groups=mesh['dp'=1,'ep'=4,'tp'=8] {'ep'}, dimensions={0} | all-to-all | bytes 2621440 | tf_op jit(solution)/shard_map/all_to_all | solution.py:37
  50.5 1.2 copy.26
  51.7 0.1 all-gather.3.cloned.1.call-update
  51.8 0.2 all-gather.5.cloned.1.call-start
  52.0 57.0 %all-gather.3.cloned.1.call-done = bf16[2,1280,2048]{2,1,0:T(8,128)(2,1)} async-done(((bf16[2,160,2048]{2,1,0:T(8,128)(2,1)}), bf16[2,1280,2048]{2,1,0:T(8,128)(2,1)}) %all-gather.3.cloned.1.call-update) | async-done | bytes 10485776 | tf_op jit(solution)/shard_map/all_gather | solution.py:38
  109.0 17.3 %fusion.6 = f32[2,1280,896]{2,1,0:T(8,128)} fusion(bf16[2,1280,2048]{2,1,0:T(8,128)(2,1)} %all-gather.3.cloned.1.call-done, bf16[2,2048,896]{2,1,0:T(8,128)(2,1)} %param.9), kind=kOutput, calls=%fused_computation.28 | convolution fusion | flops 9395240960 | bytes 27000832 | tf_op jit(solution)/shard_map/erd,edf->erf/dot_general | solution.py:39
  126.4 29.0 %convolution_convert_fusion = bf16[2,1280,2048]{2,1,0:T(8,128)(2,1)} fusion(bf16[2,896,2048]{2,1,0:T(8,128)(2,1)} %param.11, f32[2,1280,896]{2,1,0:T(8,128)} %fusion.6, bf16[2,1280,2048]{2,1,0:T(8,128)(2,1)} %all-gather.3.cloned.1.call-done, bf16[2,2048,896]{2,1,0:T(8,128)(2,1)} %param.10), kind=kOutput, calls=%fused_computation.5 | convolution fusion | flops 18809487360 | bytes 44826624 | tf_op jit(solution)/shard_map/erf,efd->erd/dot_general | solution.py:42
  155.3 10.0 %copy.27 = bf16[2,8,160,2048]{3,2,0,1:T(8,128)(2,1)} copy(bf16[2,8,160,2048]{3,2,1,0:T(8,128)(2,1)} %bitcast.50) | data formatting | bytes 20971520 | tf_op jit(solution)/shard_map/reshape | solution.py:43
  165.4 122.2 %all_to_all.36 = bf16[2,8,160,2048]{3,2,0,1:T(8,128)(2,1)} all-to-all(bf16[2,8,160,2048]{3,2,0,1:T(8,128)(2,1)} %copy.27), channel_id=1, replica_groups=mesh['dp'=1,'ep'=4,'tp'=8] {'tp'}, dimensions={1} | all-to-all | bytes 20971520 | tf_op jit(solution)/shard_map/all_to_all | solution.py:44
  287.6 0.0 copy-start
  287.6 6.4 %reduce_sum.37 = bf16[2,160,2048]{2,1,0:T(8,128)(2,1)S(1)} reduce(bf16[2,8,160,2048]{3,2,0,1:T(8,128)(2,1)} %all_to_all.36, bf16[]{:T(256)} %constant.52.clone.1), dimensions={1}, to_apply=%region_4.5 | reduce | flops 4587520 | bytes 11796482 | tf_op jit(solution)/shard_map/reduce_sum | solution.py:45
  294.1 0.1 copy.28
  294.1 20.2 %all_to_all.37 = bf16[2,4,40,2048]{3,2,0,1:T(8,128)(2,1)} all-to-all(bf16[2,4,40,2048]{3,2,0,1:T(8,128)(2,1)S(1)} %copy.28), channel_id=1, replica_groups=mesh['dp'=1,'ep'=4,'tp'=8] {'ep'}, dimensions={1} | all-to-all | bytes 2621440 | tf_op jit(solution)/shard_map/all_to_all | solution.py:46
  314.3 0.1 all-gather.5.cloned.1.call-update
  314.4 0.5 reduce_sum.35
  314.8 0.2 compare_and_fusion
  315.1 0.3 reshape.110
  315.3 0.0 copy-done
  315.3 0.2 copy.29
  315.6 54.6 %all-gather.5.cloned.1.call-done = bf16[8,320,2048]{2,1,0:T(8,128)(2,1)} async-done(((bf16[8,40,2048]{2,1,0:T(8,128)(2,1)}), bf16[8,320,2048]{2,1,0:T(8,128)(2,1)}) %all-gather.5.cloned.1.call-update) | async-done | bytes 10485776 | tf_op jit(solution)/shard_map/all_gather | solution.py:48
  370.2 21.7 %gather_fusion.1 = bf16[2048,2048]{1,0:T(8,128)(2,1)} fusion(bf16[2560,2048]{1,0:T(8,128)(2,1)} %bitcast.49, s32[2048]{0:T(1024)S(1)} %broadcast_clamp_fusion), kind=kCustom, calls=%fused_computation.1 | custom fusion | bytes 16785408 | tf_op jit(solution)/shard_map/jit(_take)/gather | solution.py:49
  391.8 14.1 %reshape.109 = bf16[1024,2,2048]{2,1,0:T(2,128)(2,1)} reshape(bf16[2048,2048]{1,0:T(8,128)(2,1)} %gather_fusion.1) | data formatting | bytes 16777216 | tf_op jit(solution)/shard_map/jit(_take)/gather | solution.py:49
  405.9 38.5 %multiply_reduce_fusion = bf16[1024,2048]{1,0:T(8,128)(2,1)} fusion(bf16[1024,2,2048]{2,1,0:T(2,128)(2,1)} %reshape.109, pred[1024,2]{1,0:T(8,128)(4,1)S(1)} %get-tuple-element.5, f32[1024,2]{1,0:T(8,128)S(1)} %copy.29), kind=kLoop, calls=%fused_computation.3 | loop fusion | flops 14680064 | bytes 12593152 | tf_op jit(solution)/shard_map/reduce_sum | solution.py:50
  (8 shorter events, 0.2 us)
Async XLA Ops:
  6.5 102.5 %all-gather.3.cloned.1.call-start = ((), (), s32[]{:S(2)}) async-start(), calls=%async_computation.3 | async-start | bytes 11796480 | tf_op jit(solution)/shard_map/all_gather | solution.py:38
  51.8 318.4 %all-gather.5.cloned.1.call-start = ((), (), s32[]{:S(2)}) async-start(), calls=%async_computation.4 | async-start | bytes 11796480 | tf_op jit(solution)/shard_map/all_gather | solution.py:48
  287.6 27.7 %copy-start = (f32[1024,2]{0,1:T(2,128)S(1)}, f32[1024,2]{0,1:T(2,128)}, u32[]{:S(2)}) copy-start(f32[1024,2]{0,1:T(2,128)} %param.8) | copy-start | bytes 24580
Sparse Core Ops, SparseCore 0:
  51.9 57.1 all-gather.2
  314.5 55.6 all-gather.4
where the time goes:
time: 452 us; the launch traced here: 451 us
  blocking collectives  166 us (37%)
  waiting for transfers between devices  112 us (25%)
  local copies, waits for them, and re-layouts  65.7 us (15%)
  other arithmetic  48.1 us (11%)
  matrix products  46.3 us (10%)
  between operations  13.6 us (3%)
    all_to_all x1, blocking collectives, device_body(): pieces = lax.all_to_all(part_out, 'tp', 1, 1, tiled=True)  122 us
    all_gather x1, waiting for transfers between devices, device_body(): gathered = lax.all_gather(arrived, 'tp', axis=1, tiled=True)  57 us
    all_gather x1, waiting for transfers between devices, device_body(): lax.all_gather(returned, 'tp', axis=1, tiled=True)  54.6 us
    reduce_sum x1, other arithmetic, device_body(): return jnp.sum(picked * gates_loc[:, :, None], axis=1).astype(jnp.bfloat16)  38.5 us
    gather x2, local copies, waits for them, and re-layouts, device_body(): picked = jnp.take(y_all, flat_slot, axis=0, mode='fill', fill_value=0)  35.7 us
    dot_general x1, matrix products, device_body(): jnp.einsum('erf,efd->erd', hidden, wd_loc, preferred_element_type=jnp.flo...  29 us
    all_to_all x1, blocking collectives, device_body(): lax.all_to_all(outgoing, 'ep', 0, 2, tiled=True)  23.3 us
    all_to_all x1, blocking collectives, device_body(): lax.all_to_all(y_mine.reshape(local_experts, n_ep, slot_share, d_model),...  20.2 us
  transfers between devices with their start and end apart: 2, of which 2 were waited for; matrix products, arithmetic and copies ran while one was open for 0% of the time, Pallas kernels for 0%

commit v1 on v0

v1 whole, which is shorter than its diff:
```python
import jax
import jax.numpy as jnp
from jax import lax
from jax.experimental import pallas as pl
from jax.experimental.pallas import tpu as pltpu
from jax.sharding import PartitionSpec as P

CAP_NUM = 5
CAP_DEN = 4
LANES = 128
MESH = pl.DeviceIdType.MESH
BF16 = jnp.bfloat16
F32 = jnp.float32


def moe_kernel(n_ep, n_tp, cap,
               ids_ref, gates_ref, x_hbm, wg_hbm, wu_hbm, wd_hbm, out_hbm,
               xv, onehot, xs, xr, w1, wd, hid, part, rv, red, ret, acc, slots, cols, colsT, yb, agb,
               x_sem, w_sem, w_send, d_send, d_recv, rs_send, rs_recv, rt_send, rt_recv,
               ag_send, ag_recv, p_send, p_recv, o_sem):
    tokens, d_model = x_hbm.shape
    n_x = n_tp // 2
    n_tile = w1.shape[1]
    half_ff = wd.shape[1]
    n_col = part.shape[3]
    half_cap = cap // 2
    half_col = n_col // 2
    ep = lax.axis_index('ep')
    tp = lax.axis_index('tp')
    core = lax.rem(tp, 2)
    xpos = tp // 2
    partner = tp + 1 - 2 * core
    yp, y2, ym = [lax.rem(ep + i, n_ep) for i in (1, 2, 3)]

    def remote(src, dst, ss, rs, ep_to, tp_to):
        return pltpu.make_async_remote_copy(src_ref=src, dst_ref=dst, send_sem=ss, recv_sem=rs,
                                            device_id={'ep': ep_to, 'tp': tp_to}, device_id_type=MESH)

    x_copy = pltpu.make_async_copy(x_hbm, xv, x_sem.at[0])
    x_copy.start()

    def lanes(i):
        return pl.ds(i * LANES, LANES)

    for i in range(n_tile):
        pltpu.make_async_copy(wg_hbm.at[core, :, lanes(i)], w1.at[0, i, :, pl.ds(0, LANES)], w_sem.at[0]).start()
        pltpu.make_async_copy(wu_hbm.at[core, :, lanes(i)], w1.at[0, i, :, pl.ds(LANES, LANES)], w_sem.at[0]).start()
    pltpu.make_async_copy(wd_hbm.at[core], wd.at[0], w_sem.at[1]).start()

    barrier = pltpu.get_barrier_semaphore()
    peers = [(ep, partner)] + [(e, t) for e in (yp, ym, y2) for t in (tp, partner)]
    peers += [(ep, lax.rem(tp + 2 * d, n_tp)) for d in range(1, n_x)]
    for e, t in peers:
        pl.semaphore_signal(barrier, inc=1, device_id={'ep': e, 'tp': t}, device_id_type=MESH)

    n_row = slots.shape[0]
    expert = lax.broadcasted_iota(jnp.int32, (n_row, LANES), 0)
    low = lax.broadcasted_iota(jnp.int32, (LANES, LANES), 0)
    high = lax.broadcasted_iota(jnp.int32, (LANES, LANES), 1)
    before = jnp.where(low < high, 1.0, 0.0).astype(BF16)
    ones = jnp.ones((LANES, LANES), BF16)
    delta = lax.rem(expert // 2 - ep + n_ep, n_ep)
    piece = jnp.where(delta == 3, 1, jnp.where(delta == 1, 2, jnp.where(delta == 2, 3, 0)))
    base = ((piece * 2 + lax.rem(expert, 2)) * cap).astype(F32)
    carry = jnp.zeros((n_row, LANES), F32)
    cols[...] = jnp.zeros_like(cols)
    for b in range(tokens // LANES):
        hit = [expert == ids_ref[j:j + 1, b * LANES:(b + 1) * LANES] for j in range(2)]
        mask = jnp.where(hit[0] | hit[1], 1.0, 0.0)
        rank = jnp.dot(mask.astype(BF16), before, preferred_element_type=F32) + carry
        carry = carry + jnp.dot(mask.astype(BF16), ones, preferred_element_type=F32)
        kept = rank < float(cap)
        slots[:, b * LANES:(b + 1) * LANES] = jnp.where((mask > 0.0) & kept, rank, -1.0)
        where_to = jnp.where(kept, base + rank + 1.0, 0.0)
        for j in range(2):
            flat = jnp.sum(jnp.where(hit[j], where_to, 0.0), axis=0, keepdims=True) - 1.0
            cols[j:j + 1, b * LANES:(b + 1) * LANES] = flat
            cols[2 + j:3 + j, b * LANES:(b + 1) * LANES] = gates_ref[j:j + 1, b * LANES:(b + 1) * LANES]

    pl.semaphore_wait(barrier, len(peers))

    other = 1 - core
    for i in range(n_tile):
        remote(wg_hbm.at[other, :, lanes(i)], w1.at[1, i, :, pl.ds(0, LANES)], w_send.at[0], w_sem.at[2], ep, partner).start()
        remote(wu_hbm.at[other, :, lanes(i)], w1.at[1, i, :, pl.ds(LANES, LANES)], w_send.at[0], w_sem.at[2], ep, partner).start()
    remote(wd_hbm.at[other], wd.at[1], w_send.at[1], w_sem.at[3], ep, partner).start()

    x_copy.wait()

    def pick(expert_id, dst):
        row = slots[pl.ds(expert_id, 1), :]
        slot = lax.broadcasted_iota(jnp.int32, (cap, tokens), 0).astype(F32)
        onehot[...] = jnp.where(slot == row, 1.0, 0.0).astype(BF16)
        step = 512
        for c in range(d_model // step):
            dst[:, c * step:(c + 1) * step] = jnp.dot(
                onehot[...], xv[:, c * step:(c + 1) * step], preferred_element_type=F32).astype(BF16)

    top, bottom = pl.ds(0, half_cap), pl.ds(half_cap, half_cap)
    sends = [
        remote(xs.at[0, top], xr.at[1, bottom], d_send.at[0], d_recv.at[1], yp, tp),
        remote(xs.at[0, bottom], xr.at[2, bottom], d_send.at[1], d_recv.at[3], yp, tp),
        remote(xs.at[1, top], xr.at[1, top], d_send.at[2], d_recv.at[0], ym, tp),
        remote(xs.at[1, bottom], xr.at[2, top], d_send.at[3], d_recv.at[2], ym, tp),
        remote(xs.at[2], xr.at[3], d_send.at[4], d_recv.at[4], y2, tp),
    ]
    pick(2 * yp + core, xs.at[0])
    sends[0].start()
    sends[1].start()
    pick(2 * ym + core, xs.at[1])
    sends[2].start()
    sends[3].start()
    pick(2 * ep + core, xr.at[0])

    def here(ref, sem):
        pltpu.make_async_copy(ref, ref, sem).wait()

    def scatter(r, d):
        c = lax.rem(xpos + d, n_x)
        return remote(part.at[r, c], rv.at[r, d - 1], rs_send.at[r, d - 1], rs_recv.at[r, d - 1], ep, 2 * c + core)

    def returns(r):
        out = []
        for k in range(2):
            t = 2 * xpos + k
            if r == 3:
                out.append(remote(red.at[3, k], ret.at[3, core], rt_send.at[3, k, 0], rt_recv.at[3, core, 0], y2, t))
            else:
                to = pl.ds((r - 1) * half_cap, half_cap)
                out.append(remote(red.at[r, k, top], ret.at[1, core, to], rt_send.at[r, k, 0],
                                  rt_recv.at[1, core, r - 1], yp, t))
                out.append(remote(red.at[r, k, bottom], ret.at[2, core, to], rt_send.at[r, k, 1],
                                  rt_recv.at[2, core, r - 1], ym, t))
        return out

    def return_own():
        return remote(red.at[0, other], ret.at[0, core], rt_send.at[0, 0, 0], rt_recv.at[0, core, 0], ep, partner)

    def finish(r):
        for d in range(1, n_x):
            scatter(r, d).wait_recv()
        total = part[r, xpos].astype(F32)
        for d in range(1, n_x):
            total = total + rv[r, d - 1].astype(F32)
        total = total.astype(BF16)
        red[r, 0] = total[:, :half_col]
        red[r, 1] = total[:, half_col:]

    def chunk(r, _):
        @pl.when(r == 1)
        def _():
            here(xr.at[1, top], d_recv.at[0])
            here(xr.at[1, bottom], d_recv.at[1])

        @pl.when(r == 2)
        def _():
            here(xr.at[2, top], d_recv.at[2])
            here(xr.at[2, bottom], d_recv.at[3])

        @pl.when(r == 3)
        def _():
            here(xr.at[3], d_recv.at[4])

        def gate_up(h, _):
            @pl.when(r == 0)
            def _():
                here(w1.at[h], w_sem.at[2 * h])

            for i in range(n_tile):
                ab = jnp.dot(xr[r], w1[h, i], preferred_element_type=F32)
                a, b = ab[:, :LANES], ab[:, LANES:]
                hid[h, :, i * LANES:(i + 1) * LANES] = (jax.nn.silu(a) * b).astype(BF16)
            return 0

        lax.fori_loop(0, 2, gate_up, 0)

        @pl.when(r == 0)
        def _():
            here(wd.at[0], w_sem.at[1])
            here(wd.at[1], w_sem.at[3])

        def down(c, _):
            step = 256
            for i in range(n_col // step):
                span = pl.ds(pl.multiple_of(c * n_col + i * step, step), step)
                o = jnp.dot(hid[0], wd[0, :, span], preferred_element_type=F32)
                o = o + jnp.dot(hid[1], wd[1, :, span], preferred_element_type=F32)
                part[r, c, :, i * step:(i + 1) * step] = o.astype(BF16)
            return 0

        lax.fori_loop(0, n_x, down, 0)
        for d in range(1, n_x):
            scatter(r, d).start()

        @pl.when(r == 0)
        def _():
            pick(2 * y2 + core, xs.at[2])
            sends[4].start()
            for b in range(tokens // LANES):
                colsT[b * LANES:(b + 1) * LANES, :] = cols[:, b * LANES:(b + 1) * LANES].T

        @pl.when(r > 0)
        def _():
            finish(r - 1)

        @pl.when(r == 1)
        def _():
            return_own().start()
            ret[0, core] = red[0, core]

        for q in (1, 2):
            @pl.when(r == q + 1)
            def _():
                for copy in returns(q):
                    copy.start()
        return 0

    lax.fori_loop(0, 4, chunk, 0)

    acc[...] = jnp.zeros_like(acc)

    def combine(q):
        rows = tokens // 4

        def block(b, _):
            at = pl.ds(pl.multiple_of(b * rows, rows), rows)
            slot = (lax.broadcasted_iota(jnp.int32, (rows, 2 * cap), 1) + q * 2 * cap).astype(F32)
            total = acc[at, :]
            for j in range(2):
                sel = jnp.where(colsT[at, j:j + 1] == slot, 1.0, 0.0).astype(BF16)
                got = jnp.dot(sel[:, :cap], ret[q, 0], preferred_element_type=F32)
                got = got + jnp.dot(sel[:, cap:], ret[q, 1], preferred_element_type=F32)
                total = total + colsT[at, 2 + j:3 + j] * got
            acc[at, :] = total
            return 0

        lax.fori_loop(0, 4, block, 0)

    here(ret.at[0, other], rt_recv.at[0, other, 0])
    combine(0)
    finish(3)
    for copy in returns(3):
        copy.start()
    for q in (1, 2):
        for k in range(2):
            for b, to in enumerate((top, bottom)):
                here(ret.at[q, k, to], rt_recv.at[q, k, b])
        combine(q)
    for k in range(2):
        here(ret.at[3, k], rt_recv.at[3, k, 0])
    combine(3)
    yb[...] = acc[...].astype(BF16)

    def block_of(t):
        return pl.ds(pl.multiple_of(t * half_col, half_col), half_col)

    def gather(d):
        return remote(yb, agb.at[d - 1], ag_send.at[d - 1], ag_recv.at[d - 1], ep, lax.rem(tp + 2 * d, n_tp))

    for d in (1, 3, 2):
        gather(d).start()

    def publish(src, t, i):
        mine = pltpu.make_async_copy(src, out_hbm.at[:, block_of(t)], o_sem.at[i])
        other_core = remote(src, out_hbm.at[:, block_of(t)], p_send.at[i], p_recv.at[i], ep, partner)
        mine.start()
        other_core.start()
        return [mine, other_core]

    pending = publish(yb, tp, 0)
    for d in (1, 3, 2):
        gather(d).wait_recv()
        pending += publish(agb.at[d - 1], lax.rem(tp + n_tp - 2 * d, n_tp), d)
    for copy in pending:
        copy.wait()

    for copy in sends:
        copy.wait_send()
    here(w1.at[1], w_send.at[0])
    here(wd.at[1], w_send.at[1])
    return_own().wait_send()
    for r in range(4):
        for d in range(1, n_x):
            scatter(r, d).wait_send()
        if r:
            for copy in returns(r):
                copy.wait_send()
    for d in range(1, n_x):
        gather(d).wait_send()


def solution(mesh):
    n_ep = mesh.shape['ep']
    n_tp = mesh.shape['tp']
    row_spec = P(('dp', 'ep'), None)

    def device_body(x_loc, ids_loc, gates_loc, wg_loc, wu_loc, wd_loc):
        tokens, d_model = x_loc.shape
        n_top = ids_loc.shape[1]
        local_experts, _, ff = wg_loc.shape
        n_experts = local_experts * n_ep
        cap = CAP_NUM * n_top * tokens // (CAP_DEN * n_experts)
        n_x = n_tp // 2
        n_col = d_model // n_x
        n_tile = ff // LANES
        vmem = pltpu.VMEM
        dma = pltpu.SemaphoreType.DMA

        def kernel(*refs):
            moe_kernel(n_ep, n_tp, cap, *refs)

        any_spec = pl.BlockSpec(memory_space=pl.ANY)
        vmem_spec = pl.BlockSpec(memory_space=pltpu.VMEM)
        return pl.pallas_call(
            kernel,
            out_shape=jax.ShapeDtypeStruct((tokens, d_model), BF16),
            in_specs=[vmem_spec, vmem_spec, any_spec, any_spec, any_spec, any_spec],
            out_specs=any_spec,
            scratch_shapes=[
                vmem((tokens, d_model), BF16),
                vmem((cap, tokens), BF16),
                vmem((3, cap, d_model), BF16),
                vmem((4, cap, d_model), BF16),
                vmem((2, n_tile, d_model, 2 * LANES), BF16),
                vmem((2, ff, d_model), BF16),
                vmem((2, cap, ff), BF16),
                vmem((4, n_x, cap, n_col), BF16),
                vmem((4, n_x - 1, cap, n_col), BF16),
                vmem((4, 2, cap, n_col // 2), BF16),
                vmem((4, 2, cap, n_col // 2), BF16),
                vmem((tokens, n_col // 2), F32),
                vmem((2 * n_experts, tokens), F32),
                vmem((LANES, tokens), F32),
                vmem((tokens, LANES), F32),
                vmem((tokens, n_col // 2), BF16),
                vmem((n_x - 1, tokens, n_col // 2), BF16),
                dma((1,)), dma((4,)), dma((2,)), dma((5,)), dma((5,)),
                dma((4, n_x - 1)), dma((4, n_x - 1)), dma((4, 2, 2)), dma((4, 2, 2)),
                dma((n_x - 1,)), dma((n_x - 1,)), dma((n_x,)), dma((n_x,)), dma((n_x,)),
            ],
            compiler_params=pltpu.CompilerParams(
                collective_id=0, has_side_effects=True, vmem_limit_bytes=63 * 1024 * 1024),
        )(ids_loc.T, gates_loc.T, x_loc, wg_loc, wu_loc, wd_loc)

    return jax.shard_map(device_body, mesh=mesh,
                         in_specs=(row_spec, row_spec, row_spec, P('ep', None, 'tp'), P('ep', None, 'tp'), P('ep', 'tp', None)),
                         out_specs=row_spec, check_vma=False)
```

time: 452 us -> 142 us (0.31)
  blocking collectives: 166 us -> 0 us
  Pallas kernels: 0 us -> 137 us
  waiting for transfers between devices: 112 us -> 0 us
  local copies, waits for them, and re-layouts: 65.7 us -> 4.79 us
  other arithmetic: 48.1 us -> 0 us
  matrix products: 46.3 us -> 0 us
  between operations: 13.6 us -> 0.01 us
    all_to_all x3 -> x0, blocking collectives: 166 us -> none  [the longest x1 122 us: device_body(): pieces = lax.all_to_all(part_out, 'tp', 1, 1, tiled=True)]
    pallas_call x0 -> x1, Pallas kernels: none -> 137 us  [device_body(): pl.pallas_call(kernel, out_shape=jax.ShapeDtypeStruct((tokens, d_model),...]
    all_gather x2 -> x0, waiting for transfers between devices: 112 us -> none  [the longest x1 57 us: device_body(): gathered = lax.all_gather(arrived, 'tp', axis=1, tiled=True)]
    dot_general x2 -> x0, matrix products: 46.3 us -> none  [the longest x1 29 us: device_body(): jnp.einsum('erf,efd->erd', hidden, wd_loc, preferred_element_type=jnp.flo...]
    reduce_sum x3 -> x0, other arithmetic: 45 us -> none  [the longest x1 38.5 us: device_body(): return jnp.sum(picked * gates_loc[:, :, None], axis=1).astype(jnp.bfloat16)]
    gather x3 -> x0, local copies, waits for them, and re-layouts: 42.9 us -> none  [the longest x2 35.7 us: device_body(): picked = jnp.take(y_all, flat_slot, axis=0, mode='fill', fill_value=0)]
    reshape x4 -> x0, local copies, waits for them, and re-layouts: 10.4 us -> none  [the longest x1 10 us: device_body(): part_out = part_out.reshape(local_experts, n_tp, n_ep * slot_share, d_model)]
    scatter x1 -> x0, local copies, waits for them, and re-layouts: 8.06 us -> none  [local_routing(): jnp.full((n_experts * capacity + 1,), tokens, jnp.int32).at[flat_slot]]
  transfers between devices with their start and end apart: 2 -> 0, of which waited for: 2 -> 0; matrix products, arithmetic and copies ran while one was open for 0% -> 0% of each run, Pallas kernels for 0% -> 0%
where the time goes in v1:
time: 142 us
  Pallas kernels  137 us (96%)
  local copies, waits for them, and re-layouts  4.79 us (3%)
    pallas_call x1, Pallas kernels, device_body(): pl.pallas_call(kernel, out_shape=jax.ShapeDtypeStruct((tokens, d_model),...  137 us
    unnamed x1, local copies, waits for them, and re-layouts  4.79 us

profile of v1, /device:TPU:97, one launch (start us, length us, event | category | flops | bytes accessed | tf_op | source)
XLA Modules:
  0.0 142.1 jit_solution(8692152705946392900)
XLA Ops:
  0.0 137.3 %shard_map.64 = bf16[1024,2048]{1,0:T(8,128)(2,1)} custom-call(s32[2,1024]{1,0:T(2,128)} %bitcast.2, f32[2,1024]{1,0:T(2,128)} %bitcast.3, bf16[1024,2048]{1,0:T(8,128)(2,1)} %refs_2_.1, bf16[2,2048,896]{2,1,0:T(8,128)(2,1)} %refs_3_.1, bf16[2,2048,896]{2,1,0:T(8,128)(2,1)} %refs_4_.1, bf16[2,896,2048]{2,1,0:T(8,128)(2,1)} %refs_5_.1), custom_call_target="tpu_custom_call" | custom-call | tf_op jit(solution)/shard_map/pallas_call | solution.py:314
  137.3 4.8 %copy.8 = bf16[1024,2048]{1,0:T(8,128)(2,1)} copy(bf16[1024,2048]{1,0:T(8,128)(2,1)} %shard_map.64) | data formatting | bytes 8388608

commit v2 on v0

v2 whole, which is shorter than its diff:
```python
import jax
import jax.numpy as jnp
from jax import lax
from jax.experimental import pallas as pl
from jax.experimental.pallas import tpu as pltpu
from jax.sharding import PartitionSpec as P

CAP_NUM = 5
CAP_DEN = 4
LANES = 128
MESH = pl.DeviceIdType.MESH
BF16 = jnp.bfloat16
F32 = jnp.float32


def moe_kernel(n_ep, n_tp, cap,
               ids_ref, gates_ref, x_hbm, wg_hbm, wu_hbm, wd_hbm, out,
               xv, onehot, xs, xr, w1, wd, hid, part, rv, red, ret, acc, slots, cols, colsT, sel,
               x_sem, w_sem, w_send, d_send, d_recv, rs_send, rs_recv, rt_send, rt_recv,
               ag_send, ag_recv, p_send, p_recv, both):
    tokens, d_model = x_hbm.shape
    n_x = n_tp // 2
    n_tile = w1.shape[1]
    unit = cap // 2
    ep = lax.axis_index('ep')
    tp = lax.axis_index('tp')
    core = lax.rem(tp, 2)
    other = 1 - core
    xpos = tp // 2
    partner = tp + 1 - 2 * core
    yp, y2, ym = [lax.rem(ep + i, n_ep) for i in (1, 2, 3)]
    right, left = lax.rem(tp + 2, n_tp), lax.rem(tp + n_tp - 2, n_tp)
    across = lax.rem(tp + 4, n_tp)

    def remote(src, dst, ss, rs, ep_to, tp_to):
        return pltpu.make_async_remote_copy(src_ref=src, dst_ref=dst, send_sem=ss, recv_sem=rs,
                                            device_id={'ep': ep_to, 'tp': tp_to}, device_id_type=MESH)

    def here(ref, sem):
        pltpu.make_async_copy(ref, ref, sem).wait()

    def lanes(i):
        return pl.ds(i * LANES, LANES)

    barrier = pltpu.get_barrier_semaphore()
    peers = [(ep, partner)] + [(e, t) for e in (yp, ym, y2) for t in (tp, partner)]
    peers += [(ep, t) for t in (right, across, left)]
    for e, t in peers:
        pl.semaphore_signal(barrier, inc=1, device_id={'ep': e, 'tp': t}, device_id_type=MESH)

    x_copy = pltpu.make_async_copy(x_hbm, xv, x_sem.at[0])
    x_copy.start()

    def move_weights(src, half, move):
        for i in range(n_tile):
            move(wg_hbm.at[src, :, lanes(i)], w1.at[half, i, :, pl.ds(0, LANES)], 0)
            move(wu_hbm.at[src, :, lanes(i)], w1.at[half, i, :, pl.ds(LANES, LANES)], 0)
        for h in range(2):
            for c in range(n_x):
                for k in range(2):
                    move(wd_hbm.at[src, :, lanes((c * 2 + k) * 2 + h)],
                         wd.at[half, h, c, :, pl.ds(k * LANES, LANES)], 1 + h)

    with jax.named_scope('routing'):
        n_row = slots.shape[0]
        expert = lax.broadcasted_iota(jnp.int32, (n_row, LANES), 0)
        low = lax.broadcasted_iota(jnp.int32, (LANES, LANES), 0)
        high = lax.broadcasted_iota(jnp.int32, (LANES, LANES), 1)
        before = jnp.where(low < high, 1.0, 0.0).astype(BF16)
        ones = jnp.ones((LANES, LANES), BF16)
        delta = lax.rem(expert // 2 - ep + n_ep, n_ep)
        piece = jnp.where(delta == 3, 1, jnp.where(delta == 1, 2, jnp.where(delta == 2, 3, 0)))
        base = (piece * 2 * cap + lax.rem(expert, 2) * unit + 1).astype(F32)
        carry = jnp.zeros((n_row, LANES), F32)
        cols[...] = jnp.zeros_like(cols)
        for b in range(tokens // LANES):
            span = slice(b * LANES, (b + 1) * LANES)
            hit = [expert == ids_ref[j:j + 1, span] for j in range(2)]
            mask = jnp.where(hit[0] | hit[1], 1.0, 0.0)
            rank = jnp.dot(mask.astype(BF16), before, preferred_element_type=F32) + carry
            carry = carry + jnp.dot(mask.astype(BF16), ones, preferred_element_type=F32)
            kept = rank < float(cap)
            slots[:, span] = jnp.where((mask > 0.0) & kept, rank, -1.0)
            where_to = jnp.where(kept, base + rank + jnp.where(rank < float(unit), 0.0, float(unit)), 0.0)
            for j in range(2):
                cols[j:j + 1, span] = jnp.sum(jnp.where(hit[j], where_to, 0.0), axis=0, keepdims=True) - 1.0
                cols[2 + j:3 + j, span] = gates_ref[j:j + 1, span]

    x_copy.wait()
    move_weights(core, 0, lambda src, dst, i: pltpu.make_async_copy(src, dst, w_sem.at[0, i]).start())


    def pick(expert_id, dst):
        with jax.named_scope('pick'):
            row = slots[pl.ds(expert_id, 1), :]
            slot = lax.broadcasted_iota(jnp.int32, (cap, tokens), 0).astype(F32)
            onehot[...] = jnp.where(slot == row, 1.0, 0.0).astype(BF16)
            step = 512
            for c in range(d_model // step):
                got = jnp.dot(onehot[...], xv[:, c * step:(c + 1) * step], preferred_element_type=F32).astype(BF16)
                for u in range(2):
                    dst[u, :, c * step:(c + 1) * step] = got[u * unit:(u + 1) * unit]

    def send_rows(i, u, land, to):
        return remote(xs.at[i, u], xr.at[land], d_send.at[i, u], d_recv.at[land], to, tp)

    near = [[send_rows(0, 0, 3, yp), send_rows(0, 1, 5, yp)], [send_rows(1, 0, 2, ym), send_rows(1, 1, 4, ym)]]
    far = [send_rows(2, 0, 6, y2), send_rows(2, 1, 7, y2)]
    pick(2 * yp + core, xs.at[0])
    with jax.named_scope('barrier'):
        pl.semaphore_wait(barrier, len(peers))
    for copy in near[0]:
        copy.start()
    move_weights(other, 1, lambda src, dst, i: remote(src, dst, w_send.at[i], w_sem.at[1, i], ep, partner).start())
    pick(2 * ym + core, xs.at[1])
    for copy in near[1]:
        copy.start()
    pick(2 * ep + core, xr.at[pl.ds(0, 2)])

    def scatter(g, u, n, h, d):
        c = lax.rem(xpos + d, n_x)
        at = pl.ds(u, n)
        return remote(part.at[at, h, c], rv.at[at, h, d - 1], rs_send.at[g, h, d - 1], rs_recv.at[g, h, d - 1],
                      ep, 2 * c + core)

    def ffn(g, u, n, first):
        rows = n * unit
        at = pl.ds(u, n)

        def gate_up(half, _):
            if first is not None:
                @pl.when(first)
                def _():
                    with jax.named_scope('wait_w1'):
                        here(w1.at[half], w_sem.at[half, 0])
            with jax.named_scope('gate_up'):
                for i in range(n_tile):
                    ab = jnp.dot(xr[at].reshape(rows, d_model), w1[half, i], preferred_element_type=F32)
                    a, b = ab[:, :LANES], ab[:, LANES:]
                    hid[half, 0:rows, i * LANES:(i + 1) * LANES] = (jax.nn.silu(a) * b).astype(BF16)
            return 0

        lax.fori_loop(0, 2, gate_up, 0)

        def down(h, _):
            if first is not None:
                @pl.when(first)
                def _():
                    with jax.named_scope('wait_wd'):
                        for half in range(2):
                            here(wd.at[half, h], w_sem.at[half, 1 + h])
            with jax.named_scope('down'):
                for c in range(n_x):
                    o = jnp.dot(hid[0, 0:rows], wd[0, h, c], preferred_element_type=F32)
                    o = o + jnp.dot(hid[1, 0:rows], wd[1, h, c], preferred_element_type=F32)
                    part[at, h, c] = o.astype(BF16).reshape(n, unit, 2 * LANES)
                for d in range(1, n_x):
                    scatter(g, u, n, h, d).start()
            return 0

        lax.fori_loop(0, 2, down, 0)

    def total(g, u, n, h):
        with jax.named_scope('wait_rs'):
            for d in range(1, n_x):
                scatter(g, u, n, h, d).wait_recv()
        with jax.named_scope('total'):
            for i in range(n):
                t = part[u + i, h, xpos].astype(F32)
                for d in range(1, n_x):
                    t = t + rv[u + i, h, d - 1].astype(F32)
                t = t.astype(BF16)
                for k in range(2):
                    red[u + i, h, k] = t[:, k * LANES:(k + 1) * LANES]

    back = {2: (yp, 1, 0), 3: (ym, 2, 0), 4: (yp, 1, 1), 5: (ym, 2, 1), 6: (y2, 3, 0), 7: (y2, 3, 1)}

    def returns(u, h):
        to, q, b = back[u]
        return [remote(red.at[u, h, k], ret.at[h, q, b, core], rt_send.at[u, h, k], rt_recv.at[h, q, b, core],
                       to, 2 * xpos + k) for k in range(2)]

    def return_own(h):
        return [remote(red.at[b, h, other], ret.at[h, 0, b, core], rt_send.at[b, h, 0], rt_recv.at[h, 0, b, core],
                       ep, partner) for b in range(2)]

    def chunk(r, _):
        for q in (1, 2):
            @pl.when(r == q)
            def _():
                with jax.named_scope('wait_rows'):
                    for u in (2 * q, 2 * q + 1):
                        here(xr.at[u], d_recv.at[u])

        ffn(r, 2 * r, 2, r == 0)

        @pl.when(r == 0)
        def _():
            pick(2 * y2 + core, xs.at[2])
            for b in range(tokens // LANES):
                colsT[b * LANES:(b + 1) * LANES, :] = cols[:, b * LANES:(b + 1) * LANES].T

        @pl.when(r == 1)
        def _():
            with jax.named_scope('near_done'):
                for copy in near[0] + near[1]:
                    copy.wait_send()
                pl.semaphore_signal(both, inc=1, device_id={'ep': ep, 'tp': partner}, device_id_type=MESH)
                pl.semaphore_wait(both, 1)
            for copy in far:
                copy.start()

        @pl.when(r > 0)
        def _():
            for h in range(2):
                total(r - 1, 2 * r - 2, 2, h)

        @pl.when(r == 1)
        def _():
            for h in range(2):
                for copy in return_own(h):
                    copy.start()
                for b in range(2):
                    ret[h, 0, b, core] = red[b, h, core]

        @pl.when(r == 2)
        def _():
            for h in range(2):
                for u in (2, 3):
                    for copy in returns(u, h):
                        copy.start()
        return 0

    lax.fori_loop(0, 3, chunk, 0)

    rows = tokens // 4
    span = 2 * unit

    def choose(at, j, first_slot, n):
        slot = (lax.broadcasted_iota(jnp.int32, (rows, n), 1) + first_slot).astype(F32)
        return jnp.where(colsT[at, j:j + 1] == slot, 1.0, 0.0).astype(BF16)

    def combine(q, b, n, fresh):
        with jax.named_scope('combine'):
            def block(i, _):
                at = pl.ds(pl.multiple_of(i * rows, rows), rows)
                t = jnp.zeros((rows, 2 * LANES), F32) if fresh else acc[at, :]
                y = jnp.concatenate([ret[h, q, pl.ds(b, n)].reshape(n * span, LANES) for h in range(2)], axis=1)
                for j in range(2):
                    got = jnp.dot(choose(at, j, q * 2 * cap + b * span, n * span), y, preferred_element_type=F32)
                    t = t + colsT[at, 2 + j:3 + j] * got
                acc[at, :] = t
                return 0

            lax.fori_loop(0, 4, block, 0)

    def wait_ret(h, q, b):
        with jax.named_scope('wait_ret'):
            for k in range(2):
                here(ret.at[h, q, b, k], rt_recv.at[h, q, b, k])

    with jax.named_scope('wait_own'):
        for h in range(2):
            for b in range(2):
                here(ret.at[h, 0, b, other], rt_recv.at[h, 0, b, other])
    combine(0, 0, 2, True)

    def tail(i, _):
        u = 6 + i
        with jax.named_scope('wait_rows'):
            here(xr.at[u], d_recv.at[u])
        ffn(3 + i, u, 1, None)

        @pl.when(i == 0)
        def _():
            for h in range(2):
                total(2, 4, 2, h)
                for w in (4, 5):
                    for copy in returns(w, h):
                        copy.start()
        return 0

    lax.fori_loop(0, 2, tail, 0)
    for h in range(2):
        total(3, 6, 1, h)
        for copy in returns(6, h):
            copy.start()

    def pick_last(i, _):
        at = pl.ds(pl.multiple_of(i * rows, rows), rows)
        for j in range(2):
            sel[j, at, :] = choose(at, j, 3 * 2 * cap + span, span)
        return 0

    lax.fori_loop(0, 4, pick_last, 0)
    for q in (1, 2):
        for h in range(2):
            for b in range(2):
                wait_ret(h, q, b)
        combine(q, 0, 2, False)
    for h in range(2):
        total(4, 7, 1, h)
        for copy in returns(7, h):
            copy.start()
    for h in range(2):
        wait_ret(h, 3, 0)
    combine(3, 0, 1, False)

    half_rows = tokens // 2

    def place(t, h, p):
        at = slice(None) if p is None else pl.ds(p * half_rows, half_rows)
        return out.at[at, pl.ds(pl.multiple_of((2 * t + h) * LANES, LANES), LANES)]

    def spread(t, h, p, to, i):
        return remote(place(t, h, p), place(t, h, p), ag_send.at[h, i], ag_recv.at[h, i], ep, to)

    def publish(t, h, p, i):
        return remote(place(t, h, p), place(t, h, p), p_send.at[h, i], p_recv.at[h, i], ep, partner)

    started = []

    def go(copy):
        copy.start()
        started.append(copy)

    for h in range(2):
        wait_ret(h, 3, 1)
        with jax.named_scope('last'):
            y = ret[h, 3, 1].reshape(span, LANES)
            for i in range(4):
                at = slice(i * rows, (i + 1) * rows)
                t = acc[at, h * LANES:(h + 1) * LANES]
                for j in range(2):
                    got = jnp.dot(sel[j, at, :], y, preferred_element_type=F32)
                    t = t + colsT[at, 2 + j:3 + j] * got
                out[at, pl.ds(pl.multiple_of((2 * tp + h) * LANES, LANES), LANES)] = t.astype(BF16)
        go(spread(tp, h, 0, right, 0))
        go(spread(tp, h, 1, left, 3))
        go(spread(tp, h, 1, right, 1))
        go(spread(tp, h, 0, left, 2))
        go(publish(tp, h, None, 0))
    with jax.named_scope('gather'):
        for h in range(2):
            spread(left, h, 0, right, 0).wait_recv()
            go(spread(left, h, 0, right, 4))
            spread(right, h, 1, left, 3).wait_recv()
            go(spread(right, h, 1, left, 5))
            go(publish(left, h, 0, 1))
            go(publish(right, h, 1, 2))
        for h in range(2):
            spread(left, h, 1, right, 1).wait_recv()
            go(publish(left, h, 1, 3))
            spread(right, h, 0, left, 2).wait_recv()
            go(publish(right, h, 0, 4))
        for h in range(2):
            spread(across, h, 0, right, 4).wait_recv()
            go(publish(across, h, 0, 5))
            spread(across, h, 1, left, 5).wait_recv()
            go(publish(across, h, 1, 6))
        for h in range(2):
            for i in range(7):
                publish(tp, h, None if i == 0 else 0, i).wait_recv()

    with jax.named_scope('drain'):
        for copy in far + started:
            copy.wait_send()
        here(w1.at[1], w_send.at[0])
        for h in range(2):
            here(wd.at[1, h], w_send.at[1 + h])
        for h in range(2):
            for copy in return_own(h):
                copy.wait_send()
            for u in back:
                for copy in returns(u, h):
                    copy.wait_send()
            for d in range(1, n_x):
                for g in range(3):
                    scatter(g, 2 * g, 2, h, d).wait_send()
                for i in range(2):
                    scatter(3 + i, 6 + i, 1, h, d).wait_send()


def solution(mesh):
    n_ep = mesh.shape['ep']
    n_tp = mesh.shape['tp']
    row_spec = P(('dp', 'ep'), None)

    def device_body(x_loc, ids_loc, gates_loc, wg_loc, wu_loc, wd_loc):
        tokens, d_model = x_loc.shape
        n_top = ids_loc.shape[1]
        local_experts, _, ff = wg_loc.shape
        n_experts = local_experts * n_ep
        cap = CAP_NUM * n_top * tokens // (CAP_DEN * n_experts)
        unit = cap // 2
        n_x = n_tp // 2
        n_tile = ff // LANES
        vmem = pltpu.VMEM
        dma = pltpu.SemaphoreType.DMA

        def kernel(*refs):
            moe_kernel(n_ep, n_tp, cap, *refs)

        any_spec = pl.BlockSpec(memory_space=pl.ANY)
        vmem_spec = pl.BlockSpec(memory_space=pltpu.VMEM)
        return pl.pallas_call(
            kernel,
            out_shape=pltpu.VMEM((tokens, d_model), BF16),
            in_specs=[vmem_spec, vmem_spec, any_spec, any_spec, any_spec, any_spec],
            out_specs=vmem_spec,
            scratch_shapes=[
                vmem((tokens, d_model), BF16),
                vmem((cap, tokens), BF16),
                vmem((3, 2, unit, d_model), BF16),
                vmem((8, unit, d_model), BF16),
                vmem((2, n_tile, d_model, 2 * LANES), BF16),
                vmem((2, 2, n_x, ff, 2 * LANES), BF16),
                vmem((2, cap, ff), BF16),
                vmem((8, 2, n_x, unit, 2 * LANES), BF16),
                vmem((8, 2, n_x - 1, unit, 2 * LANES), BF16),
                vmem((8, 2, 2, unit, LANES), BF16),
                vmem((2, 4, 2, 2, unit, LANES), BF16),
                vmem((tokens, 2 * LANES), F32),
                vmem((2 * n_experts, tokens), F32),
                vmem((LANES, tokens), F32),
                vmem((tokens, LANES), F32),
                vmem((2, tokens, 2 * unit), BF16),
                dma((1,)), dma((2, 3)), dma((3,)), dma((3, 2)), dma((8,)),
                dma((5, 2, n_x - 1)), dma((5, 2, n_x - 1)), dma((8, 2, 2)), dma((2, 4, 2, 2)),
                dma((2, 6)), dma((2, 6)), dma((2, 7)), dma((2, 7)), pltpu.SemaphoreType.REGULAR,
            ],
            compiler_params=pltpu.CompilerParams(
                collective_id=0, has_side_effects=True, vmem_limit_bytes=58 * 1024 * 1024),
        )(ids_loc.T, gates_loc.T, x_loc, wg_loc, wu_loc, wd_loc)

    return jax.shard_map(device_body, mesh=mesh,
                         in_specs=(row_spec, row_spec, row_spec, P('ep', None, 'tp'), P('ep', None, 'tp'), P('ep', 'tp', None)),
                         out_specs=row_spec, check_vma=False)
```

time: 452 us -> 110 us (0.24)
  blocking collectives: 166 us -> 0 us
  waiting for transfers between devices: 112 us -> 0 us
  Pallas kernels: 0 us -> 108 us
  local copies, waits for them, and re-layouts: 65.7 us -> 2.02 us
  other arithmetic: 48.1 us -> 0 us
  matrix products: 46.3 us -> 0 us
  between operations: 13.6 us -> 0.01 us
    all_to_all x3 -> x0, blocking collectives: 166 us -> none  [the longest x1 122 us: device_body(): pieces = lax.all_to_all(part_out, 'tp', 1, 1, tiled=True)]
    all_gather x2 -> x0, waiting for transfers between devices: 112 us -> none  [the longest x1 57 us: device_body(): gathered = lax.all_gather(arrived, 'tp', axis=1, tiled=True)]
    pallas_call x0 -> x1, Pallas kernels: none -> 108 us  [device_body(): pl.pallas_call(kernel, out_shape=pltpu.VMEM((tokens, d_model), BF16), in_...]
    dot_general x2 -> x0, matrix products: 46.3 us -> none  [the longest x1 29 us: device_body(): jnp.einsum('erf,efd->erd', hidden, wd_loc, preferred_element_type=jnp.flo...]
    reduce_sum x3 -> x0, other arithmetic: 45 us -> none  [the longest x1 38.5 us: device_body(): return jnp.sum(picked * gates_loc[:, :, None], axis=1).astype(jnp.bfloat16)]
    gather x3 -> x0, local copies, waits for them, and re-layouts: 42.9 us -> none  [the longest x2 35.7 us: device_body(): picked = jnp.take(y_all, flat_slot, axis=0, mode='fill', fill_value=0)]
    reshape x4 -> x0, local copies, waits for them, and re-layouts: 10.4 us -> none  [the longest x1 10 us: device_body(): part_out = part_out.reshape(local_experts, n_tp, n_ep * slot_share, d_model)]
    scatter x1 -> x0, local copies, waits for them, and re-layouts: 8.06 us -> none  [local_routing(): jnp.full((n_experts * capacity + 1,), tokens, jnp.int32).at[flat_slot]]
  transfers between devices with their start and end apart: 2 -> 0, of which waited for: 2 -> 0; matrix products, arithmetic and copies ran while one was open for 0% -> 0% of each run, Pallas kernels for 0% -> 0%
where the time goes in v2:
time: 110 us
  Pallas kernels  108 us (98%)
  local copies, waits for them, and re-layouts  2.02 us (2%)
    pallas_call x1, Pallas kernels, device_body(): pl.pallas_call(kernel, out_shape=pltpu.VMEM((tokens, d_model), BF16), in_...  108 us

profile of v2, /device:TPU:97, one launch (start us, length us, event | category | flops | bytes accessed | tf_op | source)
XLA Modules:
  0.0 110.2 jit_solution(8633610765281382118)
XLA Ops:
  0.0 108.2 %shard_map.64 = bf16[1024,2048]{1,0:T(8,128)(2,1)S(1)} custom-call(s32[2,1024]{1,0:T(2,128)} %bitcast.2, f32[2,1024]{1,0:T(2,128)} %bitcast.3, bf16[1024,2048]{1,0:T(8,128)(2,1)} %refs_2_.1, bf16[2,2048,896]{2,1,0:T(8,128)(2,1)} %refs_3_.1, bf16[2,2048,896]{2,1,0:T(8,128)(2,1)} %refs_4_.1, bf16[2,896,2048]{2,1,0:T(8,128)(2,1)} %refs_5_.1), custom_call_target="tpu_custom_call" | custom-call | tf_op jit(solution)/shard_map/pallas_call | solution.py:406
  108.2 2.0 %copy.8 = bf16[1024,2048]{1,0:T(8,128)(2,1)} copy(bf16[1024,2048]{1,0:T(8,128)(2,1)S(1)} %shard_map.64) | data formatting | bytes 8388608

commit v3 on v2

--- a/solution.py
+++ b/solution.py
@@ -14,10 +14,10 @@
 
 
 def moe_kernel(n_ep, n_tp, cap,
-               ids_ref, gates_ref, x_hbm, wg_hbm, wu_hbm, wd_hbm, out,
-               xv, onehot, xs, xr, w1, wd, hid, part, rv, red, ret, acc, slots, cols, colsT, sel,
+               ids_hbm, gates_hbm, x_hbm, wg_hbm, wu_hbm, wd_hbm, out,
+               ids_ref, gates_ref, xv, onehot, xs, xr, w1, wd, hid, part, rv, red, ret, acc, slots, cols, colsT, sel,
                x_sem, w_sem, w_send, d_send, d_recv, rs_send, rs_recv, rt_send, rt_recv,
-               ag_send, ag_recv, p_send, p_recv, both):
+               ag_send, ag_recv, p_send, p_recv, f_send, f_recv, both):
     tokens, d_model = x_hbm.shape
     n_x = n_tp // 2
     n_tile = w1.shape[1]
@@ -50,6 +50,9 @@
 
     x_copy = pltpu.make_async_copy(x_hbm, xv, x_sem.at[0])
     x_copy.start()
+    small = [pltpu.make_async_copy(ids_hbm, ids_ref, x_sem.at[1]), pltpu.make_async_copy(gates_hbm, gates_ref, x_sem.at[2])]
+    for copy in small:
+        copy.start()
 
     def move_weights(src, half, move):
         for i in range(n_tile):
@@ -61,6 +64,8 @@
                     move(wd_hbm.at[src, :, lanes((c * 2 + k) * 2 + h)],
                          wd.at[half, h, c, :, pl.ds(k * LANES, LANES)], 1 + h)
 
+    for copy in small:
+        copy.wait()
     with jax.named_scope('routing'):
         n_row = slots.shape[0]
         expert = lax.broadcasted_iota(jnp.int32, (n_row, LANES), 0)
@@ -104,7 +109,21 @@
     def send_rows(i, u, land, to):
         return remote(xs.at[i, u], xr.at[land], d_send.at[i, u], d_recv.at[land], to, tp)
 
-    near = [[send_rows(0, 0, 3, yp), send_rows(0, 1, 5, yp)], [send_rows(1, 0, 2, ym), send_rows(1, 1, 4, ym)]]
+    quarter = d_model // 4
+    parity = lax.rem(xpos, 2)
+
+    def columns(q):
+        return pl.ds(pl.multiple_of((2 * parity + q) * quarter, quarter), quarter)
+
+    mine = pl.ds(pl.multiple_of(2 * parity * quarter, 2 * quarter), 2 * quarter)
+
+    def send_half(i, land, to):
+        return remote(xs.at[i, 0, :, mine], xr.at[land, :, mine], d_send.at[i, 0], d_recv.at[land], to, tp)
+
+    def forward(u, q, to):
+        return remote(xr.at[u, :, columns(q)], xr.at[u, :, columns(q)], f_send.at[u - 2, q], f_recv.at[u - 2, q], ep, to)
+
+    near = [[send_half(0, 3, yp), send_rows(0, 1, 5, yp)], [send_half(1, 2, ym), send_rows(1, 1, 4, ym)]]
     far = [send_rows(2, 0, 6, y2), send_rows(2, 1, 7, y2)]
     pick(2 * yp + core, xs.at[0])
     with jax.named_scope('barrier'):
@@ -122,43 +141,6 @@
         at = pl.ds(u, n)
         return remote(part.at[at, h, c], rv.at[at, h, d - 1], rs_send.at[g, h, d - 1], rs_recv.at[g, h, d - 1],
                       ep, 2 * c + core)
-
-    def ffn(g, u, n, first):
-        rows = n * unit
-        at = pl.ds(u, n)
-
-        def gate_up(half, _):
-            if first is not None:
-                @pl.when(first)
-                def _():
-                    with jax.named_scope('wait_w1'):
-                        here(w1.at[half], w_sem.at[half, 0])
-            with jax.named_scope('gate_up'):
-                for i in range(n_tile):
-                    ab = jnp.dot(xr[at].reshape(rows, d_model), w1[half, i], preferred_element_type=F32)
-                    a, b = ab[:, :LANES], ab[:, LANES:]
-                    hid[half, 0:rows, i * LANES:(i + 1) * LANES] = (jax.nn.silu(a) * b).astype(BF16)
-            return 0
-
-        lax.fori_loop(0, 2, gate_up, 0)
-
-        def down(h, _):
-            if first is not None:
-                @pl.when(first)
-                def _():
-                    with jax.named_scope('wait_wd'):
-                        for half in range(2):
-                            here(wd.at[half, h], w_sem.at[half, 1 + h])
-            with jax.named_scope('down'):
-                for c in range(n_x):
-                    o = jnp.dot(hid[0, 0:rows], wd[0, h, c], preferred_element_type=F32)
-                    o = o + jnp.dot(hid[1, 0:rows], wd[1, h, c], preferred_element_type=F32)
-                    part[at, h, c] = o.astype(BF16).reshape(n, unit, 2 * LANES)
-                for d in range(1, n_x):
-                    scatter(g, u, n, h, d).start()
-            return 0
-
-        lax.fori_loop(0, 2, down, 0)
 
     def total(g, u, n, h):
         with jax.named_scope('wait_rs'):
@@ -180,27 +162,85 @@
         return [remote(red.at[u, h, k], ret.at[h, q, b, core], rt_send.at[u, h, k], rt_recv.at[h, q, b, core],
                        to, 2 * xpos + k) for k in range(2)]
 
-    def return_own(h):
-        return [remote(red.at[b, h, other], ret.at[h, 0, b, core], rt_send.at[b, h, 0], rt_recv.at[h, 0, b, core],
-                       ep, partner) for b in range(2)]
-
-    def chunk(r, _):
-        for q in (1, 2):
-            @pl.when(r == q)
-            def _():
-                with jax.named_scope('wait_rows'):
-                    for u in (2 * q, 2 * q + 1):
-                        here(xr.at[u], d_recv.at[u])
-
-        ffn(r, 2 * r, 2, r == 0)
-
-        @pl.when(r == 0)
-        def _():
-            pick(2 * y2 + core, xs.at[2])
-            for b in range(tokens // LANES):
-                colsT[b * LANES:(b + 1) * LANES, :] = cols[:, b * LANES:(b + 1) * LANES].T
-
-        @pl.when(r == 1)
+    def ffn(g, u, n, first=None, send=True, also=None):
+        rows = n * unit
+        at = pl.ds(u, n)
+
+        def gate_up(half, _):
+            with jax.named_scope('gate_up'):
+                for i in range(n_tile):
+                    ab = jnp.dot(xr[at].reshape(rows, d_model), w1[half, i], preferred_element_type=F32)
+                    a, b = ab[:, :LANES], ab[:, LANES:]
+                    hid[half, 0:rows, i * LANES:(i + 1) * LANES] = (jax.nn.silu(a) * b).astype(BF16)
+            return 0
+
+        if first is None:
+            lax.fori_loop(0, 2, gate_up, 0)
+        else:
+            for half in range(2):
+                with jax.named_scope('wait_w1'):
+                    here(w1.at[half], w_sem.at[half, 0])
+                gate_up(half, 0)
+                if half == 0:
+                    first()
+
+        def down(h, _):
+            if first:
+                with jax.named_scope('wait_wd'):
+                    for half in range(2):
+                        here(wd.at[half, h], w_sem.at[half, 1 + h])
+            with jax.named_scope('down'):
+                for c in range(n_x):
+                    o = jnp.dot(hid[0, 0:rows], wd[0, h, c], preferred_element_type=F32)
+                    o = o + jnp.dot(hid[1, 0:rows], wd[1, h, c], preferred_element_type=F32)
+                    part[at, h, c] = o.astype(BF16).reshape(n, unit, 2 * LANES)
+                if send:
+                    for d in range(1, n_x):
+                        scatter(g, u, n, h, d).start()
+                if also is not None:
+                    @pl.when(also)
+                    def _():
+                        for d in range(1, n_x):
+                            scatter(6, 1, 1, h, d).start()
+
+                    @pl.when(also & (h == 0))
+                    def _():
+                        for k in range(2):
+                            total(4, 6, 1, k)
+                            for copy in returns(6, k):
+                                copy.start()
+            return 0
+
+        lax.fori_loop(0, 2, down, 0)
+
+    def return_own(b, h):
+        return remote(red.at[b, h, other], ret.at[h, 0, b, core], rt_send.at[b, h, 0], rt_recv.at[h, 0, b, core],
+                      ep, partner)
+
+    def keep_own(b, h):
+        return_own(b, h).start()
+        ret[h, 0, b, core] = red[b, h, core]
+
+    def between():
+        pick(2 * y2 + core, xs.at[2])
+        for b in range(tokens // LANES):
+            colsT[b * LANES:(b + 1) * LANES, :] = cols[:, b * LANES:(b + 1) * LANES].T
+        with jax.named_scope('forward'):
+            for u in (2, 3):
+                here(xr.at[u, :, mine], d_recv.at[u])
+                forward(u, 0, right).start()
+                forward(u, 1, left).start()
+
+    ffn(0, 0, 1, first=between)
+
+    def near_unit(i, _):
+        u = 2 + i
+        with jax.named_scope('wait_rows'):
+            for q in range(2):
+                here(xr.at[u, :, columns(q)], f_recv.at[i, q])
+        ffn(1 + i, u, 1)
+
+        @pl.when(i == 0)
         def _():
             with jax.named_scope('near_done'):
                 for copy in near[0] + near[1]:
@@ -210,28 +250,24 @@
             for copy in far:
                 copy.start()
 
-        @pl.when(r > 0)
+        @pl.when(i == 1)
         def _():
             for h in range(2):
-                total(r - 1, 2 * r - 2, 2, h)
-
-        @pl.when(r == 1)
-        def _():
-            for h in range(2):
-                for copy in return_own(h):
-                    copy.start()
-                for b in range(2):
-                    ret[h, 0, b, core] = red[b, h, core]
-
-        @pl.when(r == 2)
-        def _():
-            for h in range(2):
-                for u in (2, 3):
-                    for copy in returns(u, h):
-                        copy.start()
+                total(0, 0, 1, h)
+                keep_own(0, h)
         return 0
 
-    lax.fori_loop(0, 3, chunk, 0)
+    lax.fori_loop(0, 2, near_unit, 0)
+    with jax.named_scope('wait_rows'):
+        for u in (4, 5):
+            here(xr.at[u], d_recv.at[u])
+    ffn(3, 4, 2)
+    ffn(6, 1, 1, send=False)
+    for u in (2, 3):
+        for h in range(2):
+            total(u - 1, u, 1, h)
+            for copy in returns(u, h):
+                copy.start()
 
     rows = tokens // 4
     span = 2 * unit
@@ -259,49 +295,59 @@
             for k in range(2):
                 here(ret.at[h, q, b, k], rt_recv.at[h, q, b, k])
 
-    with jax.named_scope('wait_own'):
-        for h in range(2):
-            for b in range(2):
-                here(ret.at[h, 0, b, other], rt_recv.at[h, 0, b, other])
-    combine(0, 0, 2, True)
+    def wait_own(h, b):
+        with jax.named_scope('wait_own'):
+            here(ret.at[h, 0, b, other], rt_recv.at[h, 0, b, other])
+
+    for h in range(2):
+        wait_own(h, 0)
+    combine(0, 0, 1, True)
+
+    def pick_last(i, _):
+        at = pl.ds(pl.multiple_of(i * rows, rows), rows)
+        for j in range(2):
+            for w, q in enumerate((3, 0)):
+                sel[j, at, w * span:(w + 1) * span] = choose(at, j, q * 2 * cap + span, span)
+        return 0
 
     def tail(i, _):
         u = 6 + i
         with jax.named_scope('wait_rows'):
             here(xr.at[u], d_recv.at[u])
-        ffn(3 + i, u, 1, None)
+        ffn(4 + i, u, 1, also=i == 1)
 
         @pl.when(i == 0)
         def _():
+            lax.fori_loop(0, 4, pick_last, 0)
             for h in range(2):
-                total(2, 4, 2, h)
+                total(3, 4, 2, h)
                 for w in (4, 5):
                     for copy in returns(w, h):
                         copy.start()
         return 0
 
     lax.fori_loop(0, 2, tail, 0)
-    for h in range(2):
-        total(3, 6, 1, h)
-        for copy in returns(6, h):
-            copy.start()
-
-    def pick_last(i, _):
-        at = pl.ds(pl.multiple_of(i * rows, rows), rows)
-        for j in range(2):
-            sel[j, at, :] = choose(at, j, 3 * 2 * cap + span, span)
-        return 0
-
-    lax.fori_loop(0, 4, pick_last, 0)
-    for q in (1, 2):
+
+    def combine_near(q):
         for h in range(2):
             for b in range(2):
                 wait_ret(h, q, b)
         combine(q, 0, 2, False)
-    for h in range(2):
-        total(4, 7, 1, h)
+
+    def last_far(h):
+        total(5, 7, 1, h)
         for copy in returns(7, h):
             copy.start()
+
+    def last_own(h):
+        total(6, 1, 1, h)
+        keep_own(1, h)
+
+    combine_near(1)
+    last_far(0)
+    combine_near(2)
+    last_own(0)
+    last_far(1)
     for h in range(2):
         wait_ret(h, 3, 0)
     combine(3, 0, 1, False)
@@ -324,10 +370,11 @@
         copy.start()
         started.append(copy)
 
-    for h in range(2):
+    def finish(h):
+        wait_own(h, 1)
         wait_ret(h, 3, 1)
         with jax.named_scope('last'):
-            y = ret[h, 3, 1].reshape(span, LANES)
+            y = jnp.concatenate([ret[h, 3, 1].reshape(span, LANES), ret[h, 0, 1].reshape(span, LANES)], axis=0)
             for i in range(4):
                 at = slice(i * rows, (i + 1) * rows)
                 t = acc[at, h * LANES:(h + 1) * LANES]
@@ -340,14 +387,22 @@
         go(spread(tp, h, 1, right, 1))
         go(spread(tp, h, 0, left, 2))
         go(publish(tp, h, None, 0))
-    with jax.named_scope('gather'):
-        for h in range(2):
+
+    def relay(h):
+        with jax.named_scope('relay'):
             spread(left, h, 0, right, 0).wait_recv()
             go(spread(left, h, 0, right, 4))
             spread(right, h, 1, left, 3).wait_recv()
             go(spread(right, h, 1, left, 5))
             go(publish(left, h, 0, 1))
             go(publish(right, h, 1, 2))
+
+    finish(0)
+    last_own(1)
+    finish(1)
+    relay(0)
+    relay(1)
+    with jax.named_scope('gather'):
         for h in range(2):
             spread(left, h, 1, right, 1).wait_recv()
             go(publish(left, h, 1, 3))
@@ -366,19 +421,20 @@
         for copy in far + started:
             copy.wait_send()
         here(w1.at[1], w_send.at[0])
+        for u in (2, 3):
+            forward(u, 0, right).wait_send()
+            forward(u, 1, left).wait_send()
         for h in range(2):
             here(wd.at[1, h], w_send.at[1 + h])
         for h in range(2):
-            for copy in return_own(h):
-                copy.wait_send()
+            for b in range(2):
+                return_own(b, h).wait_send()
             for u in back:
                 for copy in returns(u, h):
                     copy.wait_send()
             for d in range(1, n_x):
-                for g in range(3):
-                    scatter(g, 2 * g, 2, h, d).wait_send()
-                for i in range(2):
-                    scatter(3 + i, 6 + i, 1, h, d).wait_send()
+                for g, u, n in ((0, 0, 1), (1, 2, 1), (2, 3, 1), (3, 4, 2), (4, 6, 1), (5, 7, 1), (6, 1, 1)):
+                    scatter(g, u, n, h, d).wait_send()
 
 
 def solution(mesh):
@@ -406,9 +462,11 @@
         return pl.pallas_call(
             kernel,
             out_shape=pltpu.VMEM((tokens, d_model), BF16),
-            in_specs=[vmem_spec, vmem_spec, any_spec, any_spec, any_spec, any_spec],
+            in_specs=[any_spec] * 6,
             out_specs=vmem_spec,
             scratch_shapes=[
+                vmem(ids_loc.shape[::-1], jnp.int32),
+                vmem(gates_loc.shape[::-1], F32),
                 vmem((tokens, d_model), BF16),
                 vmem((cap, tokens), BF16),
                 vmem((3, 2, unit, d_model), BF16),
@@ -424,10 +482,11 @@
                 vmem((2 * n_experts, tokens), F32),
                 vmem((LANES, tokens), F32),
                 vmem((tokens, LANES), F32),
-                vmem((2, tokens, 2 * unit), BF16),
-                dma((1,)), dma((2, 3)), dma((3,)), dma((3, 2)), dma((8,)),
-                dma((5, 2, n_x - 1)), dma((5, 2, n_x - 1)), dma((8, 2, 2)), dma((2, 4, 2, 2)),
-                dma((2, 6)), dma((2, 6)), dma((2, 7)), dma((2, 7)), pltpu.SemaphoreType.REGULAR,
+                vmem((2, tokens, 4 * unit), BF16),
+                dma((3,)), dma((2, 3)), dma((3,)), dma((3, 2)), dma((8,)),
+                dma((7, 2, n_x - 1)), dma((7, 2, n_x - 1)), dma((8, 2, 2)), dma((2, 4, 2, 2)),
+                dma((2, 6)), dma((2, 6)), dma((2, 7)), dma((2, 7)), dma((2, 2)), dma((2, 2)),
+                pltpu.SemaphoreType.REGULAR,
             ],
             compiler_params=pltpu.CompilerParams(
                 collective_id=0, has_side_effects=True, vmem_limit_bytes=58 * 1024 * 1024),

time: 110 us -> 108 us (0.982)
  Pallas kernels: 108 us -> 106 us
    pallas_call x1, Pallas kernels: 108 us -> 106 us  [device_body(): pl.pallas_call(kernel, out_shape=pltpu.VMEM((tokens, d_model), BF16), in_...]
where the time goes in v3:
time: 108 us
  Pallas kernels  106 us (98%)
  local copies, waits for them, and re-layouts  2.02 us (2%)
    pallas_call x1, Pallas kernels, device_body(): pl.pallas_call(kernel, out_shape=pltpu.VMEM((tokens, d_model), BF16), in_...  106 us

profile of v3, /device:TPU:97, one launch (start us, length us, event | category | flops | bytes accessed | tf_op | source)
XLA Modules:
  0.0 108.1 jit_solution(14300962294202619098)
XLA Ops:
  0.0 106.1 %shard_map.64 = bf16[1024,2048]{1,0:T(8,128)(2,1)S(1)} custom-call(s32[2,1024]{1,0:T(2,128)} %bitcast.2, f32[2,1024]{1,0:T(2,128)} %bitcast.3, bf16[1024,2048]{1,0:T(8,128)(2,1)} %refs_2_.1, bf16[2,2048,896]{2,1,0:T(8,128)(2,1)} %refs_3_.1, bf16[2,2048,896]{2,1,0:T(8,128)(2,1)} %refs_4_.1, bf16[2,896,2048]{2,1,0:T(8,128)(2,1)} %refs_5_.1), custom_call_target="tpu_custom_call" | custom-call | tf_op jit(solution)/shard_map/pallas_call | solution.py:462
  106.1 2.0 %copy.8 = bf16[1024,2048]{1,0:T(8,128)(2,1)} copy(bf16[1024,2048]{1,0:T(8,128)(2,1)S(1)} %shard_map.64) | data formatting | bytes 8388608

commit v4 on v3

--- a/solution.py
+++ b/solution.py
@@ -17,7 +17,7 @@
                ids_hbm, gates_hbm, x_hbm, wg_hbm, wu_hbm, wd_hbm, out,
                ids_ref, gates_ref, xv, onehot, xs, xr, w1, wd, hid, part, rv, red, ret, acc, slots, cols, colsT, sel,
                x_sem, w_sem, w_send, d_send, d_recv, rs_send, rs_recv, rt_send, rt_recv,
-               ag_send, ag_recv, p_send, p_recv, f_send, f_recv, both):
+               ag_send, ag_recv, p_send, p_recv, f_send, f_recv, h_send, h_recv, both):
     tokens, d_model = x_hbm.shape
     n_x = n_tp // 2
     n_tile = w1.shape[1]
@@ -117,13 +117,19 @@
 
     mine = pl.ds(pl.multiple_of(2 * parity * quarter, 2 * quarter), 2 * quarter)
 
-    def send_half(i, land, to):
-        return remote(xs.at[i, 0, :, mine], xr.at[land, :, mine], d_send.at[i, 0], d_recv.at[land], to, tp)
-
-    def forward(u, q, to):
-        return remote(xr.at[u, :, columns(q)], xr.at[u, :, columns(q)], f_send.at[u - 2, q], f_recv.at[u - 2, q], ep, to)
-
-    near = [[send_half(0, 3, yp), send_rows(0, 1, 5, yp)], [send_half(1, 2, ym), send_rows(1, 1, 4, ym)]]
+    def strip(p):
+        return pl.ds(p * (unit // 2), unit // 2)
+
+    def send_half(i, land, to, p):
+        return remote(xs.at[i, 0, strip(p), mine], xr.at[land, strip(p), mine],
+                      h_send.at[i, p], h_recv.at[land - 2, p], to, tp)
+
+    def forward(u, p, q, to):
+        at = xr.at[u, strip(p), columns(q)]
+        return remote(at, at, f_send.at[u - 2, p, q], f_recv.at[u - 2, p, q], ep, to)
+
+    near = [[send_half(0, 3, yp, 0), send_half(0, 3, yp, 1), send_rows(0, 1, 5, yp)],
+            [send_half(1, 2, ym, 0), send_half(1, 2, ym, 1), send_rows(1, 1, 4, ym)]]
     far = [send_rows(2, 0, 6, y2), send_rows(2, 1, 7, y2)]
     pick(2 * yp + core, xs.at[0])
     with jax.named_scope('barrier'):
@@ -198,17 +204,10 @@
                     for d in range(1, n_x):
                         scatter(g, u, n, h, d).start()
                 if also is not None:
-                    @pl.when(also)
+                    @pl.when(also == (h == 1))
                     def _():
                         for d in range(1, n_x):
                             scatter(6, 1, 1, h, d).start()
-
-                    @pl.when(also & (h == 0))
-                    def _():
-                        for k in range(2):
-                            total(4, 6, 1, k)
-                            for copy in returns(6, k):
-                                copy.start()
             return 0
 
         lax.fori_loop(0, 2, down, 0)
@@ -226,18 +225,20 @@
         for b in range(tokens // LANES):
             colsT[b * LANES:(b + 1) * LANES, :] = cols[:, b * LANES:(b + 1) * LANES].T
         with jax.named_scope('forward'):
-            for u in (2, 3):
-                here(xr.at[u, :, mine], d_recv.at[u])
-                forward(u, 0, right).start()
-                forward(u, 1, left).start()
+            for p in range(2):
+                for u in (2, 3):
+                    here(xr.at[u, strip(p), mine], h_recv.at[u - 2, p])
+                    forward(u, p, 0, right).start()
+                    forward(u, p, 1, left).start()
 
     ffn(0, 0, 1, first=between)
 
     def near_unit(i, _):
         u = 2 + i
         with jax.named_scope('wait_rows'):
-            for q in range(2):
-                here(xr.at[u, :, columns(q)], f_recv.at[i, q])
+            for p in range(2):
+                for q in range(2):
+                    here(xr.at[u, strip(p), columns(q)], f_recv.at[i, p, q])
         ffn(1 + i, u, 1)
 
         @pl.when(i == 0)
@@ -343,6 +344,10 @@
         total(6, 1, 1, h)
         keep_own(1, h)
 
+    for h in range(2):
+        total(4, 6, 1, h)
+        for copy in returns(6, h):
+            copy.start()
     combine_near(1)
     last_far(0)
     combine_near(2)
@@ -422,8 +427,9 @@
             copy.wait_send()
         here(w1.at[1], w_send.at[0])
         for u in (2, 3):
-            forward(u, 0, right).wait_send()
-            forward(u, 1, left).wait_send()
+            for p in range(2):
+                forward(u, p, 0, right).wait_send()
+                forward(u, p, 1, left).wait_send()
         for h in range(2):
             here(wd.at[1, h], w_send.at[1 + h])
         for h in range(2):
@@ -485,7 +491,7 @@
                 vmem((2, tokens, 4 * unit), BF16),
                 dma((3,)), dma((2, 3)), dma((3,)), dma((3, 2)), dma((8,)),
                 dma((7, 2, n_x - 1)), dma((7, 2, n_x - 1)), dma((8, 2, 2)), dma((2, 4, 2, 2)),
-                dma((2, 6)), dma((2, 6)), dma((2, 7)), dma((2, 7)), dma((2, 2)), dma((2, 2)),
+                dma((2, 6)), dma((2, 6)), dma((2, 7)), dma((2, 7)), dma((2, 2, 2)), dma((2, 2, 2)), dma((2, 2)), dma((2, 2)),
                 pltpu.SemaphoreType.REGULAR,
             ],
             compiler_params=pltpu.CompilerParams(

time: 108 us -> 105 us (0.972)
  Pallas kernels: 106 us -> 103 us
    pallas_call x1, Pallas kernels: 106 us -> 103 us  [device_body(): pl.pallas_call(kernel, out_shape=pltpu.VMEM((tokens, d_model), BF16), in_...]
where the time goes in v4:
time: 105 us
  Pallas kernels  103 us (98%)
  local copies, waits for them, and re-layouts  2.02 us (2%)
    pallas_call x1, Pallas kernels, device_body(): pl.pallas_call(kernel, out_shape=pltpu.VMEM((tokens, d_model), BF16), in_...  103 us

profile of v4, /device:TPU:97, one launch (start us, length us, event | category | flops | bytes accessed | tf_op | source)
XLA Modules:
  0.0 104.7 jit_solution(1767864915634671082)
XLA Ops:
  0.0 102.7 %shard_map.64 = bf16[1024,2048]{1,0:T(8,128)(2,1)S(1)} custom-call(s32[2,1024]{1,0:T(2,128)} %bitcast.2, f32[2,1024]{1,0:T(2,128)} %bitcast.3, bf16[1024,2048]{1,0:T(8,128)(2,1)} %refs_2_.1, bf16[2,2048,896]{2,1,0:T(8,128)(2,1)} %refs_3_.1, bf16[2,2048,896]{2,1,0:T(8,128)(2,1)} %refs_4_.1, bf16[2,896,2048]{2,1,0:T(8,128)(2,1)} %refs_5_.1), custom_call_target="tpu_custom_call" | custom-call | tf_op jit(solution)/shard_map/pallas_call | solution.py:468
  102.7 2.0 %copy.8 = bf16[1024,2048]{1,0:T(8,128)(2,1)} copy(bf16[1024,2048]{1,0:T(8,128)(2,1)S(1)} %shard_map.64) | data formatting | bytes 8388608

commit v5 on v4

--- a/solution.py
+++ b/solution.py
@@ -17,7 +17,7 @@
                ids_hbm, gates_hbm, x_hbm, wg_hbm, wu_hbm, wd_hbm, out,
                ids_ref, gates_ref, xv, onehot, xs, xr, w1, wd, hid, part, rv, red, ret, acc, slots, cols, colsT, sel,
                x_sem, w_sem, w_send, d_send, d_recv, rs_send, rs_recv, rt_send, rt_recv,
-               ag_send, ag_recv, p_send, p_recv, f_send, f_recv, h_send, h_recv, both):
+               ag_send, ag_recv, p_send, p_recv, f_send, f_recv, h_recv, both):
     tokens, d_model = x_hbm.shape
     n_x = n_tp // 2
     n_tile = w1.shape[1]
@@ -106,9 +106,6 @@
                 for u in range(2):
                     dst[u, :, c * step:(c + 1) * step] = got[u * unit:(u + 1) * unit]
 
-    def send_rows(i, u, land, to):
-        return remote(xs.at[i, u], xr.at[land], d_send.at[i, u], d_recv.at[land], to, tp)
-
     quarter = d_model // 4
     parity = lax.rem(xpos, 2)
 
@@ -122,21 +119,27 @@
 
     def send_half(i, land, to, p):
         return remote(xs.at[i, 0, strip(p), mine], xr.at[land, strip(p), mine],
-                      h_send.at[i, p], h_recv.at[land - 2, p], to, tp)
+                      d_send.at[0], h_recv.at[p], to, tp)
+
+    def send_near(i, land, to):
+        return remote(xs.at[i, 1], xr.at[land], d_send.at[0], d_recv.at[0], to, tp)
+
+    def send_far(u):
+        return remote(xs.at[2, u], xr.at[6 + u], d_send.at[1], d_recv.at[1 + u], y2, tp)
 
     def forward(u, p, q, to):
         at = xr.at[u, strip(p), columns(q)]
-        return remote(at, at, f_send.at[u - 2, p, q], f_recv.at[u - 2, p, q], ep, to)
-
-    near = [[send_half(0, 3, yp, 0), send_half(0, 3, yp, 1), send_rows(0, 1, 5, yp)],
-            [send_half(1, 2, ym, 0), send_half(1, 2, ym, 1), send_rows(1, 1, 4, ym)]]
-    far = [send_rows(2, 0, 6, y2), send_rows(2, 1, 7, y2)]
+        return remote(at, at, f_send.at[0], f_recv.at[u - 2], ep, to)
+
+    near = [[send_half(0, 3, yp, 0), send_half(0, 3, yp, 1), send_near(0, 5, yp)],
+            [send_half(1, 2, ym, 0), send_half(1, 2, ym, 1), send_near(1, 4, ym)]]
+    far = [send_far(0), send_far(1)]
     pick(2 * yp + core, xs.at[0])
     with jax.named_scope('barrier'):
         pl.semaphore_wait(barrier, len(peers))
     for copy in near[0]:
         copy.start()
-    move_weights(other, 1, lambda src, dst, i: remote(src, dst, w_send.at[i], w_sem.at[1, i], ep, partner).start())
+    move_weights(other, 1, lambda src, dst, i: remote(src, dst, w_send.at[min(i, 1)], w_sem.at[1, i], ep, partner).start())
     pick(2 * ym + core, xs.at[1])
     for copy in near[1]:
         copy.start()
@@ -145,13 +148,12 @@
     def scatter(g, u, n, h, d):
         c = lax.rem(xpos + d, n_x)
         at = pl.ds(u, n)
-        return remote(part.at[at, h, c], rv.at[at, h, d - 1], rs_send.at[g, h, d - 1], rs_recv.at[g, h, d - 1],
+        return remote(part.at[at, h, c], rv.at[at, h, d - 1], rs_send.at[0], rs_recv.at[g, h],
                       ep, 2 * c + core)
 
     def total(g, u, n, h):
         with jax.named_scope('wait_rs'):
-            for d in range(1, n_x):
-                scatter(g, u, n, h, d).wait_recv()
+            here(rv.at[pl.ds(u, n), h], rs_recv.at[g, h])
         with jax.named_scope('total'):
             for i in range(n):
                 t = part[u + i, h, xpos].astype(F32)
@@ -165,7 +167,8 @@
 
     def returns(u, h):
         to, q, b = back[u]
-        return [remote(red.at[u, h, k], ret.at[h, q, b, core], rt_send.at[u, h, k], rt_recv.at[h, q, b, core],
+        sem = q - 1 if q < 3 else 2 + b * (1 + h)
+        return [remote(red.at[u, h, k], ret.at[h, q, b, core], rt_send.at[0], rt_recv.at[sem],
                        to, 2 * xpos + k) for k in range(2)]
 
     def ffn(g, u, n, first=None, send=True, also=None):
@@ -213,7 +216,7 @@
         lax.fori_loop(0, 2, down, 0)
 
     def return_own(b, h):
-        return remote(red.at[b, h, other], ret.at[h, 0, b, core], rt_send.at[b, h, 0], rt_recv.at[h, 0, b, core],
+        return remote(red.at[b, h, other], ret.at[h, 0, b, core], rt_send.at[0], rt_recv.at[5 + b * (1 + h)],
                       ep, partner)
 
     def keep_own(b, h):
@@ -226,8 +229,8 @@
             colsT[b * LANES:(b + 1) * LANES, :] = cols[:, b * LANES:(b + 1) * LANES].T
         with jax.named_scope('forward'):
             for p in range(2):
+                here(xr.at[pl.ds(2, 2), strip(p), mine], h_recv.at[p])
                 for u in (2, 3):
-                    here(xr.at[u, strip(p), mine], h_recv.at[u - 2, p])
                     forward(u, p, 0, right).start()
                     forward(u, p, 1, left).start()
 
@@ -236,16 +239,14 @@
     def near_unit(i, _):
         u = 2 + i
         with jax.named_scope('wait_rows'):
-            for p in range(2):
-                for q in range(2):
-                    here(xr.at[u, strip(p), columns(q)], f_recv.at[i, p, q])
+            theirs = pl.ds(pl.multiple_of(2 * (1 - parity) * quarter, 2 * quarter), 2 * quarter)
+            here(xr.at[u, :, theirs], f_recv.at[i])
         ffn(1 + i, u, 1)
 
         @pl.when(i == 0)
         def _():
             with jax.named_scope('near_done'):
-                for copy in near[0] + near[1]:
-                    copy.wait_send()
+                here(xr.at[pl.ds(0, 3)], d_send.at[0])
                 pl.semaphore_signal(both, inc=1, device_id={'ep': ep, 'tp': partner}, device_id_type=MESH)
                 pl.semaphore_wait(both, 1)
             for copy in far:
@@ -260,8 +261,7 @@
 
     lax.fori_loop(0, 2, near_unit, 0)
     with jax.named_scope('wait_rows'):
-        for u in (4, 5):
-            here(xr.at[u], d_recv.at[u])
+        here(xr.at[pl.ds(4, 2)], d_recv.at[0])
     ffn(3, 4, 2)
     ffn(6, 1, 1, send=False)
     for u in (2, 3):
@@ -291,17 +291,11 @@
 
             lax.fori_loop(0, 4, block, 0)
 
-    def wait_ret(h, q, b):
+    def wait_ret(ref, i):
         with jax.named_scope('wait_ret'):
-            for k in range(2):
-                here(ret.at[h, q, b, k], rt_recv.at[h, q, b, k])
-
-    def wait_own(h, b):
-        with jax.named_scope('wait_own'):
-            here(ret.at[h, 0, b, other], rt_recv.at[h, 0, b, other])
-
-    for h in range(2):
-        wait_own(h, 0)
+            here(ref, rt_recv.at[i])
+
+    wait_ret(ret.at[:, 0, 0, other], 5)
     combine(0, 0, 1, True)
 
     def pick_last(i, _):
@@ -314,7 +308,7 @@
     def tail(i, _):
         u = 6 + i
         with jax.named_scope('wait_rows'):
-            here(xr.at[u], d_recv.at[u])
+            here(xr.at[u], d_recv.at[1 + i])
         ffn(4 + i, u, 1, also=i == 1)
 
         @pl.when(i == 0)
@@ -330,9 +324,7 @@
     lax.fori_loop(0, 2, tail, 0)
 
     def combine_near(q):
-        for h in range(2):
-            for b in range(2):
-                wait_ret(h, q, b)
+        wait_ret(ret.at[:, q], q - 1)
         combine(q, 0, 2, False)
 
     def last_far(h):
@@ -353,8 +345,7 @@
     combine_near(2)
     last_own(0)
     last_far(1)
-    for h in range(2):
-        wait_ret(h, 3, 0)
+    wait_ret(ret.at[:, 3, 0], 2)
     combine(3, 0, 1, False)
 
     half_rows = tokens // 2
@@ -364,20 +355,17 @@
         return out.at[at, pl.ds(pl.multiple_of((2 * t + h) * LANES, LANES), LANES)]
 
     def spread(t, h, p, to, i):
-        return remote(place(t, h, p), place(t, h, p), ag_send.at[h, i], ag_recv.at[h, i], ep, to)
-
-    def publish(t, h, p, i):
-        return remote(place(t, h, p), place(t, h, p), p_send.at[h, i], p_recv.at[h, i], ep, partner)
-
-    started = []
+        return remote(place(t, h, p), place(t, h, p), ag_send.at[0], ag_recv.at[h, i], ep, to)
+
+    def publish(t, h, p):
+        return remote(place(t, h, p), place(t, h, p), p_send.at[0], p_recv.at[0], ep, partner)
 
     def go(copy):
         copy.start()
-        started.append(copy)
 
     def finish(h):
-        wait_own(h, 1)
-        wait_ret(h, 3, 1)
+        wait_ret(ret.at[h, 0, 1, other], 6 + h)
+        wait_ret(ret.at[h, 3, 1], 3 + h)
         with jax.named_scope('last'):
             y = jnp.concatenate([ret[h, 3, 1].reshape(span, LANES), ret[h, 0, 1].reshape(span, LANES)], axis=0)
             for i in range(4):
@@ -391,7 +379,7 @@
         go(spread(tp, h, 1, left, 3))
         go(spread(tp, h, 1, right, 1))
         go(spread(tp, h, 0, left, 2))
-        go(publish(tp, h, None, 0))
+        go(publish(tp, h, None))
 
     def relay(h):
         with jax.named_scope('relay'):
@@ -399,8 +387,8 @@
             go(spread(left, h, 0, right, 4))
             spread(right, h, 1, left, 3).wait_recv()
             go(spread(right, h, 1, left, 5))
-            go(publish(left, h, 0, 1))
-            go(publish(right, h, 1, 2))
+            go(publish(left, h, 0))
+            go(publish(right, h, 1))
 
     finish(0)
     last_own(1)
@@ -410,37 +398,25 @@
     with jax.named_scope('gather'):
         for h in range(2):
             spread(left, h, 1, right, 1).wait_recv()
-            go(publish(left, h, 1, 3))
+            go(publish(left, h, 1))
             spread(right, h, 0, left, 2).wait_recv()
-            go(publish(right, h, 0, 4))
+            go(publish(right, h, 0))
         for h in range(2):
             spread(across, h, 0, right, 4).wait_recv()
-            go(publish(across, h, 0, 5))
+            go(publish(across, h, 0))
             spread(across, h, 1, left, 5).wait_recv()
-            go(publish(across, h, 1, 6))
-        for h in range(2):
-            for i in range(7):
-                publish(tp, h, None if i == 0 else 0, i).wait_recv()
+            go(publish(across, h, 1))
+        here(out.at[:, pl.ds(0, 8 * LANES)], p_recv.at[0])
 
     with jax.named_scope('drain'):
-        for copy in far + started:
-            copy.wait_send()
+        here(xs.at[2], d_send.at[1])
         here(w1.at[1], w_send.at[0])
-        for u in (2, 3):
-            for p in range(2):
-                forward(u, p, 0, right).wait_send()
-                forward(u, p, 1, left).wait_send()
-        for h in range(2):
-            here(wd.at[1, h], w_send.at[1 + h])
-        for h in range(2):
-            for b in range(2):
-                return_own(b, h).wait_send()
-            for u in back:
-                for copy in returns(u, h):
-                    copy.wait_send()
-            for d in range(1, n_x):
-                for g, u, n in ((0, 0, 1), (1, 2, 1), (2, 3, 1), (3, 4, 2), (4, 6, 1), (5, 7, 1), (6, 1, 1)):
-                    scatter(g, u, n, h, d).wait_send()
+        here(wd.at[1], w_send.at[1])
+        here(xr.at[0], f_send.at[0])
+        here(rv, rs_send.at[0])
+        here(red.at[pl.ds(0, 7)], rt_send.at[0])
+        here(out.at[:, pl.ds(0, 6 * LANES)], ag_send.at[0])
+        here(out.at[:, pl.ds(0, 8 * LANES)], p_send.at[0])
 
 
 def solution(mesh):
@@ -489,9 +465,9 @@
                 vmem((LANES, tokens), F32),
                 vmem((tokens, LANES), F32),
                 vmem((2, tokens, 4 * unit), BF16),
-                dma((3,)), dma((2, 3)), dma((3,)), dma((3, 2)), dma((8,)),
-                dma((7, 2, n_x - 1)), dma((7, 2, n_x - 1)), dma((8, 2, 2)), dma((2, 4, 2, 2)),
-                dma((2, 6)), dma((2, 6)), dma((2, 7)), dma((2, 7)), dma((2, 2, 2)), dma((2, 2, 2)), dma((2, 2)), dma((2, 2)),
+                dma((3,)), dma((2, 3)), dma((2,)), dma((2,)), dma((3,)),
+                dma((1,)), dma((7, 2)), dma((1,)), dma((8,)),
+                dma((1,)), dma((2, 6)), dma((1,)), dma((1,)), dma((1,)), dma((2,)), dma((2,)),
                 pltpu.SemaphoreType.REGULAR,
             ],
             compiler_params=pltpu.CompilerParams(

time: 105 us -> 103 us (0.981)
  Pallas kernels: 103 us -> 101 us
    pallas_call x1, Pallas kernels: 103 us -> 101 us  [device_body(): pl.pallas_call(kernel, out_shape=pltpu.VMEM((tokens, d_model), BF16), in_...]
where the time goes in v5:
time: 103 us
  Pallas kernels  101 us (98%)
  local copies, waits for them, and re-layouts  2.02 us (2%)
    pallas_call x1, Pallas kernels, device_body(): pl.pallas_call(kernel, out_shape=pltpu.VMEM((tokens, d_model), BF16), in_...  101 us

profile of v5, /device:TPU:97, one launch (start us, length us, event | category | flops | bytes accessed | tf_op | source)
XLA Modules:
  0.0 102.9 jit_solution(5675935759417260065)
XLA Ops:
  0.0 100.9 %shard_map.64 = bf16[1024,2048]{1,0:T(8,128)(2,1)S(1)} custom-call(s32[2,1024]{1,0:T(2,128)} %bitcast.2, f32[2,1024]{1,0:T(2,128)} %bitcast.3, bf16[1024,2048]{1,0:T(8,128)(2,1)} %refs_2_.1, bf16[2,2048,896]{2,1,0:T(8,128)(2,1)} %refs_3_.1, bf16[2,2048,896]{2,1,0:T(8,128)(2,1)} %refs_4_.1, bf16[2,896,2048]{2,1,0:T(8,128)(2,1)} %refs_5_.1), custom_call_target="tpu_custom_call" | custom-call | tf_op jit(solution)/shard_map/pallas_call | solution.py:444
  100.9 2.0 %copy.8 = bf16[1024,2048]{1,0:T(8,128)(2,1)} copy(bf16[1024,2048]{1,0:T(8,128)(2,1)S(1)} %shard_map.64) | data formatting | bytes 8388608

commit v6 on v5

--- a/solution.py
+++ b/solution.py
@@ -375,7 +375,8 @@
                     got = jnp.dot(sel[j, at, :], y, preferred_element_type=F32)
                     t = t + colsT[at, 2 + j:3 + j] * got
                 out[at, pl.ds(pl.multiple_of((2 * tp + h) * LANES, LANES), LANES)] = t.astype(BF16)
-        go(spread(tp, h, 0, right, 0))
+                if i == 1:
+                    go(spread(tp, h, 0, right, 0))
         go(spread(tp, h, 1, left, 3))
         go(spread(tp, h, 1, right, 1))
         go(spread(tp, h, 0, left, 2))

time: 103 us -> 103 us (level)
  no operation moved by 1% of the time
where the time goes in v6:
time: 103 us
  Pallas kernels  101 us (98%)
  local copies, waits for them, and re-layouts  2.02 us (2%)
    pallas_call x1, Pallas kernels, device_body(): pl.pallas_call(kernel, out_shape=pltpu.VMEM((tokens, d_model), BF16), in_...  101 us

profile of v6, /device:TPU:97, one launch (start us, length us, event | category | flops | bytes accessed | tf_op | source)
XLA Modules:
  0.0 102.9 jit_solution(8339624617367018714)
XLA Ops:
  0.0 100.8 %shard_map.64 = bf16[1024,2048]{1,0:T(8,128)(2,1)S(1)} custom-call(s32[2,1024]{1,0:T(2,128)} %bitcast.2, f32[2,1024]{1,0:T(2,128)} %bitcast.3, bf16[1024,2048]{1,0:T(8,128)(2,1)} %refs_2_.1, bf16[2,2048,896]{2,1,0:T(8,128)(2,1)} %refs_3_.1, bf16[2,2048,896]{2,1,0:T(8,128)(2,1)} %refs_4_.1, bf16[2,896,2048]{2,1,0:T(8,128)(2,1)} %refs_5_.1), custom_call_target="tpu_custom_call" | custom-call | tf_op jit(solution)/shard_map/pallas_call | solution.py:445
  100.8 2.0 %copy.8 = bf16[1024,2048]{1,0:T(8,128)(2,1)} copy(bf16[1024,2048]{1,0:T(8,128)(2,1)S(1)} %shard_map.64) | data formatting | bytes 8388608
